TPU v7x, 256 devices: a whole 4x4x8 slice. The times are simulated.
256 devices in a mesh: col: 32 (over z, y), row: 8 (over x, core).
Axes of the slice: x: 4, y: 4, z: 8, core: 2. Of those that a mesh axis runs over, the one named last changes fastest.
Arguments:
- img_emb: bfloat16 [32768, 1024], P(('row', 'col'))
- txt_emb: bfloat16 [32768, 1024], P(('row', 'col'))
- log_scale: float32 [], replicated
Outputs:
- output 1: float32 [], replicated
- output 2: bfloat16 [32768, 1024], P(('row', 'col'))
- output 3: bfloat16 [32768, 1024], P(('row', 'col'))
- output 4: float32 [], replicated
All inputs are finite; a program needn't handle non-finite values.
Results may differ from a plain program's by a relative error of at most 0.001.
Values are sent between devices in bfloat16 or wider.
A program may use at most 768 MiB of HBM per device.

v0:
```python
import jax
import jax.numpy as jnp
from jax import lax
from jax.sharding import PartitionSpec as P, NamedSharding


def solution(mesh):
    n_row = mesh.shape["row"]
    n_col = mesh.shape["col"]
    batch_spec = P(("row", "col"), None)
    both_axes = ("row", "col")

    def local_tile(img_loc, txt_loc, log_scale):
        rows_dev = img_loc.shape[0]
        batch_size = rows_dev * n_row * n_col
        inv_count = 1.0 / (2 * batch_size)
        row_id = lax.axis_index("row")
        col_id = lax.axis_index("col")
        logit_scale = jnp.exp(log_scale)
        img_block = lax.all_gather(img_loc, "col", tiled=True)
        txt_block = lax.all_gather(txt_loc, "row", tiled=True)
        logits = logit_scale * jnp.einsum("id,jd->ij", img_block, txt_block, preferred_element_type=jnp.float32)
        row_glob = row_id * (rows_dev * n_col) + jnp.arange(rows_dev * n_col)
        col_pos = jnp.arange(rows_dev * n_row)
        col_glob = ((col_pos // rows_dev) * n_col + col_id) * rows_dev + col_pos % rows_dev
        diag_mask = row_glob[:, None] == col_glob[None, :]
        row_max = jnp.max(logits, axis=1)
        row_exp = jnp.exp(logits - row_max[:, None])
        row_part = jnp.sum(row_exp, axis=1)
        col_max = jnp.max(logits, axis=0)
        col_exp = jnp.exp(logits - col_max[None, :])
        col_part = jnp.sum(col_exp, axis=0)
        row_top = lax.pmax(row_max, "col")
        row_tot = lax.psum(row_part * jnp.exp(row_max - row_top), "col")
        row_lse = row_top + jnp.log(row_tot)
        col_top = lax.pmax(col_max, "row")
        col_tot = lax.psum(col_part * jnp.exp(col_max - col_top), "row")
        col_lse = col_top + jnp.log(col_tot)
        own_block = lax.dynamic_slice(logits, (col_id * rows_dev, row_id * rows_dev), (rows_dev, rows_dev))
        own_diag = jnp.diagonal(own_block)
        own_row_lse = lax.dynamic_slice(row_lse, (col_id * rows_dev,), (rows_dev,))
        own_col_lse = lax.dynamic_slice(col_lse, (row_id * rows_dev,), (rows_dev,))
        loss_part = jnp.sum(own_row_lse + own_col_lse - 2.0 * own_diag)
        total_loss = lax.psum(loss_part, both_axes) * inv_count
        row_factor = jnp.exp(row_max - row_lse) * inv_count
        col_factor = jnp.exp(col_max - col_lse) * inv_count
        grad_tile = row_exp * row_factor[:, None] + col_exp * col_factor[None, :] - jnp.where(diag_mask, 2.0 * inv_count, 0.0)
        d_log_scale = lax.psum(jnp.sum(grad_tile * logits), both_axes)
        grad_bf = grad_tile.astype(jnp.bfloat16)
        img_part = jnp.einsum("ij,jd->id", grad_bf, txt_block, preferred_element_type=jnp.float32)
        img_sum = lax.psum_scatter(img_part, "col", scatter_dimension=0, tiled=True)
        d_img = (logit_scale * img_sum).astype(jnp.bfloat16)
        txt_part = jnp.einsum("ij,id->jd", grad_bf, img_block, preferred_element_type=jnp.float32)
        txt_sum = lax.psum_scatter(txt_part, "row", scatter_dimension=0, tiled=True)
        d_txt = (logit_scale * txt_sum).astype(jnp.bfloat16)
        return total_loss, d_img, d_txt, d_log_scale

    return jax.shard_map(local_tile, mesh=mesh, in_specs=(batch_spec, batch_spec, P()), out_specs=(P(), batch_spec, batch_spec, P()), check_vma=False)
```

profile of v0, /device:TPU:1, one launch (start us, length us, event | category | flops | bytes accessed | tf_op | source)
XLA Modules:
  0.0 791.3 jit_solution(15794441525069719678)
XLA Ops:
  7.2 0.0 all-gather.5.cloned.1.call-start
  7.2 0.7 all-gather.5.cloned.1.call-update
  7.9 0.0 all-gather.3.cloned.1.call-start
  7.9 0.7 all-gather.3.cloned.1.call-update
  8.6 0.0 reduce-scatter.5.cloned.1.call-start
  9.4 32.5 %all-gather.5.cloned.1.call-done = bf16[1024,1024]{1,0:T(8,128)(2,1)} async-done(((bf16[128,1024]{1,0:T(8,128)(2,1)}), bf16[1024,1024]{1,0:T(8,128)(2,1)}) %all-gather.5.cloned.1.call-update) | async-done | bytes 2097168 | tf_op jit(solution)/shard_map/all_gather | solution.py:21
  41.9 99.5 %all-gather.3.cloned.1.call-done = bf16[4096,1024]{1,0:T(8,128)(2,1)} async-done(((bf16[128,1024]{1,0:T(8,128)(2,1)}), bf16[4096,1024]{1,0:T(8,128)(2,1)}) %all-gather.3.cloned.1.call-update) | async-done | bytes 8388624 | tf_op jit(solution)/shard_map/all_gather | solution.py:20
  141.4 16.7 %fusion.14 = (f32[4096]{0:T(1024)S(1)}, f32[1024]{0:T(1024)S(1)}, f32[4096,1024]{1,0:T(8,128)}) fusion(bf16[4096,1024]{1,0:T(8,128)(2,1)} %all-gather.3.cloned.1.call-done, bf16[1024,1024]{1,0:T(8,128)(2,1)} %all-gather.5.cloned.1.call-done, f32[]{:T(128)S(6)} %exp.21), kind=kOutput, calls=%fused_computation.35 | convolution fusion | flops 8602512384 | bytes 27283460 | tf_op jit(solution)/shard_map/id,jd->ij/dot_general | solution.py:22
  158.1 13.2 %pmax.15 = f32[1024]{0:T(1024)S(1)} all-reduce(f32[1024]{0:T(1024)S(1)} %get-tuple-element.7), channel_id=1, replica_groups=mesh['col'=32,'row'=8] {'row'}, use_global_device_ids=true, to_apply=%region_5.6 | all-reduce | flops 1024 | bytes 8192 | tf_op jit(solution)/shard_map/pmax | solution.py:36
  171.3 111.8 %pmax.14 = f32[4096]{0:T(1024)S(1)} all-reduce(f32[4096]{0:T(1024)S(1)} %get-tuple-element.6), channel_id=1, replica_groups=mesh['col'=32,'row'=8] {'col'}, use_global_device_ids=true, to_apply=%region_1.2 | all-reduce | flops 4096 | bytes 32768 | tf_op jit(solution)/shard_map/pmax | solution.py:33
  283.2 9.1 %fusion = (f32[4096]{0:T(1024)S(1)}, f32[1024]{0:T(1024)S(1)}) fusion(f32[4096,1024]{1,0:T(8,128)} %get-tuple-element.16, f32[4096]{0:T(1024)S(1)} %get-tuple-element.6, f32[1024]{0:T(1024)S(1)} %get-tuple-element.7), kind=kLoop, calls=%fused_computation.5 | loop fusion | flops 16772096 | bytes 16818176 | tf_op jit(solution)/shard_map/reduce_sum | solution.py:29
  292.3 41.2 %psum.29 = f32[1024]{0:T(1024)S(1)} all-reduce(f32[1024]{0:T(1024)S(1)} %exponential_multiply_fusion.3), channel_id=1, replica_groups=mesh['col'=32,'row'=8] {'row'}, use_global_device_ids=true, to_apply=%region_7.8 | all-reduce | flops 1024 | bytes 8192 | tf_op jit(solution)/shard_map/psum | solution.py:37
  333.5 110.1 %psum.28 = f32[4096]{0:T(1024)S(1)} all-reduce(f32[4096]{0:T(1024)S(1)} %exponential_multiply_fusion.1), channel_id=1, replica_groups=mesh['col'=32,'row'=8] {'col'}, use_global_device_ids=true, to_apply=%region_3.4 | all-reduce | flops 4096 | bytes 32768 | tf_op jit(solution)/shard_map/psum | solution.py:34
  443.6 14.4 %fusion.2 = (bf16[4096,1024]{1,0:T(8,128)(2,1)S(1)}, f32[]{:T(128)}) fusion(f32[4096,1024]{1,0:T(8,128)} %get-tuple-element.16, s32[1024]{0:T(1024)S(1)} %fusion.12, f32[1024]{0:T(1024)S(1)} %get-tuple-element.12, f32[4096]{0:T(1024)S(1)} %get-tuple-element.10, f32[1024]{0:T(1024)S(1)} %get-tuple-element.7, f32[4096]{0:T(1024)S(1)} %get-tuple-element.6, ...), kind=kLoop, calls=%fused_computation.7 | loop fusion | flops 46137344 | bytes 25227268 | tf_op jit(solution)/shard_map/convert_element_type | solution.py:49
  458.0 0.0 copy-start
  458.0 3.2 copy-done
  461.2 0.0 copy-start.1
  461.2 12.7 %fusion.16 = f32[1024,1024]{1,0:T(8,128)} fusion(bf16[4096,1024]{1,0:T(8,128)(2,1)S(1)} %get-tuple-element.14, bf16[4096,1024]{1,0:T(8,128)(2,1)} %all-gather.3.cloned.1.call-done), kind=kOutput, calls=%fused_computation.37 | convolution fusion | flops 8589934592 | bytes 20971520 | tf_op jit(solution)/shard_map/ij,id->jd/dot_general | solution.py:53
  474.0 0.0 reduce-scatter.5.cloned.1.call-update
  474.0 0.0 reduce-scatter.3.cloned.1.call-start
  474.0 0.0 copy-done.1
  474.1 14.5 %fusion.15 = f32[4096,1024]{1,0:T(8,128)} fusion(bf16[4096,1024]{1,0:T(8,128)(2,1)} %copy-done, bf16[1024,1024]{1,0:T(8,128)(2,1)S(1)} %copy-done.1), kind=kOutput, calls=%fused_computation.36 | convolution fusion | flops 8589934592 | bytes 27262976 | tf_op jit(solution)/shard_map/ij,jd->id/dot_general | solution.py:50
  488.5 0.0 reduce-scatter.3.cloned.1.call-update
  488.6 0.9 dynamic_slice.11
  489.4 1.2 gather_fusion
  490.7 0.7 subtract_reduce_fusion
  491.4 100.2 %all-reduce = (f32[]{:T(128)}, f32[]{:T(128)}) all-reduce(f32[]{:T(128)} %subtract_reduce_fusion, f32[]{:T(128)} %get-tuple-element.15), channel_id=1, replica_groups=mesh['col'=32,'row'=8] {'row','col'}, use_global_device_ids=true, to_apply=%region_9.10 | all-reduce | flops 2 | bytes 16 | tf_op jit(solution)/shard_map/psum | solution.py:44
  592.2 0.0 reduce-scatter.5.cloned.1.call-done
  592.3 1.8 multiply_convert_fusion
  594.1 187.8 %reduce-scatter.3.cloned.1.call-done = f32[128,1024]{1,0:T(8,128)} async-done(((f32[4096,1024]{1,0:T(8,128)}), f32[128,1024]{1,0:T(8,128)}) %reduce-scatter.3.cloned.1.call-update) | async-done | bytes 524304 | tf_op jit(solution)/shard_map/reduce_scatter | solution.py:51
  781.8 1.8 multiply_convert_fusion.1
  (7 shorter events, 0.1 us)
Async XLA Ops:
  7.2 34.7 %all-gather.5.cloned.1.call-start = ((), (), s32[]{:S(2)}) async-start(), calls=%async_computation.3 | async-start | bytes 2359296 | tf_op jit(solution)/shard_map/all_gather | solution.py:21
  7.9 133.5 %all-gather.3.cloned.1.call-start = ((), (), s32[]{:S(2)}) async-start(), calls=%async_computation.2 | async-start | bytes 8650752 | tf_op jit(solution)/shard_map/all_gather | solution.py:20
  8.6 583.6 %reduce-scatter.5.cloned.1.call-start = ((), (), s32[]{:S(2)}) async-start(), calls=%async_computation.5 | async-start | bytes 4718592 | tf_op jit(solution)/shard_map/reduce_scatter | solution.py:54
  458.0 3.2 copy-start
  461.2 12.8 %copy-start.1 = (bf16[1024,1024]{1,0:T(8,128)(2,1)S(1)}, bf16[1024,1024]{1,0:T(8,128)(2,1)}, u32[]{:S(2)}) copy-start(bf16[1024,1024]{1,0:T(8,128)(2,1)} %all-gather.5.cloned.1.call-done) | copy-start | bytes 6291460
  474.0 307.9 %reduce-scatter.3.cloned.1.call-start = ((), (), s32[]{:S(2)}) async-start(), calls=%async_computation.4 | async-start | bytes 17301504 | tf_op jit(solution)/shard_map/reduce_scatter | solution.py:51
Sparse Core Ops, SparseCore 0:
  9.8 32.0 all-gather.4
  44.5 96.8 all-gather.2
  474.1 61.1 reduce-scatter.4
  539.2 242.5 reduce-scatter.2
where the time goes:
time: 795 us; the launch traced here: 791 us
  blocking collectives  377 us (47%)
  waiting for transfers between devices  321 us (40%)
  matrix products  43.9 us (6%)
  other arithmetic  27.9 us (4%)
  between operations  16.3 us (2%)
    reduce_scatter x1, waiting for transfers between devices, local_tile(): img_sum = lax.psum_scatter(img_part, 'col', scatter_dimension=0, tiled=True)  188 us
    pmax x1, blocking collectives, local_tile(): row_top = lax.pmax(row_max, 'col')  112 us
    psum x1, blocking collectives, local_tile(): row_tot = lax.psum(row_part * jnp.exp(row_max - row_top), 'col')  110 us
    psum x1, blocking collectives, local_tile(): total_loss = lax.psum(loss_part, both_axes) * inv_count  100 us
    all_gather x1, waiting for transfers between devices, local_tile(): img_block = lax.all_gather(img_loc, 'col', tiled=True)  99.5 us
    psum x1, blocking collectives, local_tile(): col_tot = lax.psum(col_part * jnp.exp(col_max - col_top), 'row')  41.2 us
    all_gather x1, waiting for transfers between devices, local_tile(): txt_block = lax.all_gather(txt_loc, 'row', tiled=True)  32.5 us
    dot_general x1, matrix products, local_tile(): jnp.einsum('id,jd->ij', img_block, txt_block, preferred_element_type=jnp....  16.7 us
  transfers between devices with their start and end apart: 4, of which 3 were waited for; matrix products, arithmetic and copies ran while one was open for 2% of the time, Pallas kernels for 0%

commit v1 on v0

v1 whole, which is shorter than its diff:
```python
import functools

import jax
import jax.numpy as jnp
from jax import lax
from jax.experimental import pallas as pl
from jax.experimental.pallas import tpu as pltpu
from jax.sharding import PartitionSpec as P

MESH = pl.DeviceIdType.MESH
F32 = jnp.float32
BF16 = jnp.bfloat16
W = 128


class Names:
    def __init__(self):
        self.ids = {}

    def __call__(self, *key, count=1):
        if key not in self.ids:
            self.ids[key] = sum(c for _, c in self.ids.values()), count
        return self.ids[key][0]


N_SEM = 224


def kernel(NX, NY, NZ, NC, scale_ref, img_ref, txt_ref, dimg_ref, dtxt_ref, scal_ref,
           iall, tall, imgt, ee, gb, rsum, rel, csum, cel, rall, call_, uref, vref, ub, sc1, sc2,
           recv1, recv2, prt, zrecv, ssem, rsem):
    D = img_ref.shape[1]
    NI, NT = NX * NY, NZ * NC
    XY, ZC = NI > 1, NT > 1
    H, Q = D // 2, D // 4
    inv = 1.0 / (2.0 * W * NI * NT)
    row, col = lax.axis_index("row"), lax.axis_index("col")
    x, c = lax.div(row, NC), lax.rem(row, NC)
    z, y = lax.div(col, NY), lax.rem(col, NY)
    mxy, mzc = x * NY + y, z * NC + c
    scale = scale_ref[0, 0]
    rx = lambda v: lax.rem(v + 2 * NX, NX)
    ry = lambda v: lax.rem(v + 2 * NY, NY)
    rz = lambda v: lax.rem(v + 2 * NZ, NZ)

    def dev(px, py, pz, pc):
        return (pz * NY + py, px * NC + pc)

    plane = [(p, rx(x + p // NY), ry(y + p % NY)) for p in range(1, NI)]
    line = [(p, rz(z + p // NC), lax.rem(c + p % NC, NC)) for p in range(1, NT)]
    barrier = pltpu.get_barrier_semaphore()
    for _, px, py in plane:
        pl.semaphore_signal(barrier, inc=1, device_id=dev(px, py, z, c), device_id_type=MESH)
    for _, pz, pc in line:
        pl.semaphore_signal(barrier, inc=1, device_id=dev(x, y, pz, pc), device_id_type=MESH)
    iall[x, y] = img_ref[...]
    tall[z, c] = txt_ref[...]
    csum[...] = jnp.zeros_like(csum)
    cel[...] = jnp.zeros_like(cel)
    pl.semaphore_wait(barrier, len(plane) + len(line))

    rid, sid = Names(), Names()
    sends = []

    def send(src, dst, key, device, dyn=None):
        n = rid(*key) if dyn is None else rid(key[0], count=16) + dyn
        copy = pltpu.make_async_remote_copy(
            src_ref=src, dst_ref=dst, send_sem=ssem.at[sid(*key)], recv_sem=rsem.at[n],
            device_id=device, device_id_type=MESH)
        copy.start()
        sends.append(copy)

    def got(dst, key, dyn=None):
        n = rid(*key) if dyn is None else rid(key[0], count=16) + dyn
        pltpu.make_async_remote_copy(
            src_ref=dst, dst_ref=dst, send_sem=ssem.at[0], recv_sem=rsem.at[n],
            device_id=dev(x, y, z, c), device_id_type=MESH).wait_recv()

    sg = (1, -1)
    lo, full = W // 4, W // 2

    def rows(half, part=None):
        start, size = half * full, full
        if part is not None:
            start, size = start + part * lo, lo
        return pl.ds(start, size)

    def first_dev(half, d):
        return dev(rx(x + sg[d]), y, z, c) if half == 0 else dev(x, ry(y + sg[d]), z, c)

    def second_dev(half, d):
        return dev(x, ry(y + sg[d]), z, c) if half == 0 else dev(rx(x + sg[d]), y, z, c)

    def first_piece(half, off):
        return (rx(x + off), y) if half == 0 else (x, ry(y + off))

    def second_piece(half, off1, off2):
        return (rx(x + off1), ry(y + off2)) if half == 0 else (rx(x + off2), ry(y + off1))

    def ipc(pc, sl):
        return iall.at[pc[0], pc[1], sl]

    def first_send(half, d, t):
        if t == 1:
            ref = img_ref.at[rows(half)]
            send(ref, ipc((x, y), rows(half)), ("f", half, d, 1), first_dev(half, d))
        else:
            ref = ipc(first_piece(half, -sg[d]), rows(half, d))
            send(ref, ref, ("f", half, d, 2), first_dev(half, d))

    def first_got(half, d, t):
        got(ipc(first_piece(half, -sg[d] * t), rows(half) if t == 1 else rows(half, d)), ("f", half, d, t))

    def second_send(half, off, d, t):
        if t == 1:
            ref = ipc(second_piece(half, off, 0), rows(half))
            src = img_ref.at[rows(half)] if off == 0 else ref
            send(src, ref, ("s", half, off, d, 1), second_dev(half, d))
        else:
            ref = ipc(second_piece(half, off, -sg[d]), rows(half, d))
            send(ref, ref, ("s", half, off, d, 2), second_dev(half, d))

    def second_got(half, off, d, t):
        got(ipc(second_piece(half, off, -sg[d] * t), rows(half) if t == 1 else rows(half, d)), ("s", half, off, d, t))

    def t_send(d, t, h):
        ref = tall.at[rz(z - sg[d] * (t - 1)), c, rows(h)]
        src = txt_ref.at[rows(h)] if t == 1 else ref
        send(src, ref, ("t", d, t, h), dev(x, y, rz(z + sg[d]), c))

    def t_got(d, t, h):
        got(tall.at[rz(z - sg[d] * t), c, rows(h)], ("t", d, t, h))

    def t_pass(off):
        ref = tall.at[rz(z + off), c]
        send(txt_ref if off == 0 else ref, ref, ("p", off), dev(x, y, z, 1 - c))

    def t_passed(off):
        got(tall.at[rz(z + off), 1 - c], ("p", off))

    both = (0, 1)
    if XY:
        for half in both:
            for d in both:
                first_send(half, d, 1)
    if ZC:
        for h in both:
            for d in both:
                t_send(d, 1, h)
        t_pass(0)
    if XY:
        for half in both:
            for d in both:
                second_send(half, 0, d, 1)
        for d in both:
            for half in both:
                first_got(half, d, 1)
                first_send(half, d, 2)
        for d in both:
            for half in both:
                for e in both:
                    second_send(half, -sg[d], e, 1)
    if ZC:
        for h in both:
            for d in both:
                t_got(d, 1, h)
                t_send(d, 2, h)
        t_pass(-1)
        t_pass(1)
    if XY:
        for d in both:
            for half in both:
                second_got(half, 0, d, 1)
                second_send(half, 0, d, 2)
        for d in both:
            for half in both:
                first_got(half, d, 2)
        for half in both:
            for d in both:
                second_send(half, 2, d, 1)
    if ZC:
        for h in both:
            for d in both:
                t_got(d, 2, h)
                t_send(d, 3, h)
        t_pass(-2)
        t_pass(2)
    if XY:
        for off in (-1, 1):
            for d in both:
                for half in both:
                    second_got(half, off, d, 1)
                    second_send(half, off, d, 2)
    if ZC:
        for h in both:
            for d in both:
                t_got(d, 3, h)
                if h == d:
                    t_send(d, 4, h)
        t_pass(-3)
        t_pass(3)
    if XY:
        for d in both:
            for half in both:
                second_got(half, 2, d, 1)
                second_send(half, 2, d, 2)
    if ZC:
        for d in both:
            t_got(d, 4, d)
        t_pass(4)
    if XY:
        for off in (0, -1, 1, 2):
            for d in both:
                for half in both:
                    second_got(half, off, d, 2)
    if ZC:
        for off in (0, -1, 1, -2, 2, -3, 3, 4):
            t_passed(off)

    CW = NC * W

    def logits_rows(i, carry):
        lhs = iall[i].reshape(NY * W, D)
        for zz in range(NZ):
            rhs = tall[zz].reshape(CW, D)
            dots = lax.dot_general(lhs, rhs, (((1,), (1,)), ((), ())), preferred_element_type=F32)
            lg = dots * scale
            e = jnp.exp(lg)
            el = e * lg
            ee[i, 0:NY, :, zz * CW:(zz + 1) * CW] = e.reshape(NY, W, CW)
            for ref, val in ((rsum, e), (rel, el)):
                part = val[:, :W]
                for k in range(1, NC):
                    part = part + val[:, k * W:(k + 1) * W]
                part = part.reshape(NY, W, W)
                ref[i] = part if zz == 0 else ref[i] + part
            for ref, val in ((csum, e), (cel, el)):
                ref[:, zz * CW:(zz + 1) * CW] += jnp.sum(val.reshape(NY * W // 8, 8, CW), axis=0)
        return carry

    lax.fori_loop(0, NX, logits_rows, 0)

    for k in range(NI):
        rall[mxy, k:k + 1, :] = jnp.sum(jnp.transpose(rsum[k // NY, k % NY]), axis=0, keepdims=True)
    for k in range(NT):
        call_[mzc, k:k + 1, :] = jnp.sum(csum[:, k * W:(k + 1) * W], axis=0, keepdims=True)

    def share(buf, key, peers, me, to):
        for p in peers:
            send(buf.at[me], buf.at[me], (key, p[0]), to(p), dyn=me)

    def shared(buf, key, peers, slot):
        for p in peers:
            got(buf.at[slot(p)], (key,), dyn=slot(p))
        total = buf[0]
        for k in range(1, len(peers) + 1):
            total = total + buf[k]
        return total

    to_plane = lambda p: dev(p[1], p[2], z, c)
    to_line = lambda p: dev(x, y, p[1], p[2])
    plane_slot = lambda p: p[1] * NY + p[2]
    line_slot = lambda p: p[1] * NC + p[2]
    share(rall, "r", plane, mxy, to_plane)
    share(call_, "c", line, mzc, to_line)
    for k in range(NI):
        tr = jnp.transpose(iall[k // NY, k % NY])
        for d in both:
            imgt[d, :, k * W:(k + 1) * W] = tr[d * H:(d + 1) * H]
    prod = img_ref[...].astype(F32) * txt_ref[...].astype(F32)
    pos = prod[:, :W]
    for k in range(1, D // W):
        pos = pos + prod[:, k * W:(k + 1) * W]
    pos = scale * jnp.sum(pos, axis=0, keepdims=True)
    rtot = shared(rall, "r", plane, plane_slot)
    uref[...] = rtot
    ctot = shared(call_, "c", line, line_slot)
    vref[...] = ctot
    loss = jnp.log(uref[pl.ds(mxy, 1), :]) + jnp.log(vref[pl.ds(mzc, 1), :]) - 2.0 * pos
    u, v = inv / rtot, inv / ctot
    uref[...] = u
    vref[...] = v

    dts = jnp.zeros((8, W), F32)
    for k in range(NT):
        dts = dts + cel[:, k * W:(k + 1) * W] * v[k:k + 1, :]
    for k in range(NI):
        ub[k // NY, k % NY] = jnp.transpose(jnp.broadcast_to(u[k:k + 1, :], (W, W)))

    def grad_rows(i, acc):
        for j in range(NY):
            uu = ub[i, j]
            acc = acc + jnp.sum((uu * rel[i, j]).reshape(W // 8, 8, W), axis=0)
            for k in range(NT):
                sl = slice(k * W, (k + 1) * W)
                gb[i, j, :, sl] = (ee[i, j, :, sl] * (uu + vref[k:k + 1, :])).astype(BF16)
        return acc

    dts = lax.fori_loop(0, NX, grad_rows, dts)
    own = pl.ds(pl.multiple_of(mzc * W, W), W)
    eye = lax.broadcasted_iota(jnp.int32, (W, W), 0) == lax.broadcasted_iota(jnp.int32, (W, W), 1)
    gb[x, y, :, own] = (ee[x, y, :, own] * (ub[x, y] + vref[pl.ds(mzc, 1), :])
                        - jnp.where(eye, 2.0 * inv, 0.0)).astype(BF16)
    dt_part = jnp.sum(dts, axis=0, keepdims=True) - (2.0 * inv) * pos
    line_no = lax.broadcasted_iota(jnp.int32, (8, W), 0)
    sc1[mxy] = jnp.where(line_no == 0, jnp.broadcast_to(loss * inv, (8, W)),
                         jnp.where(line_no == 1, jnp.broadcast_to(dt_part, (8, W)), 0.0))
    share(sc1, "m", plane, mxy, to_plane)

    def unit_t(s):
        def body(d, carry):
            zz = rz(z - (1 - 2 * d) * (s + 1))
            rhs = gb[:, :, :, pl.ds(pl.multiple_of(zz * CW, W), CW)].reshape(NI * W, CW)
            res = jnp.dot(imgt[d], rhs, preferred_element_type=F32)
            for k in range(NC):
                ee[d * 2 + k, :, :, 1024 + s * W:1024 + (s + 1) * W] = res[:, k * W:(k + 1) * W].reshape(4, W, W)
            return carry

        lax.fori_loop(0, 2, body, 0)

    def unit_i(j):
        for first in both:
            def body(d, carry):
                q = first * 2 + d
                step = (1 - 2 * d) * (j + 1)
                lhs = gb[:, ry(y - step)] if first == 0 else gb[rx(x - step)]
                rhs = tall[:, :, :, pl.ds(pl.multiple_of(q * Q, W), Q)].reshape(NT * W, Q)
                res = jnp.dot(lhs.reshape(4 * W, NT * W), rhs, preferred_element_type=F32)
                ee[q, :, :, j * Q:(j + 1) * Q] = res.reshape(4, W, Q)
                return carry

            lax.fori_loop(0, 2, body, 0)

    def sub(n):
        return pl.ds(n * 2, 2)

    def i_dev(q, d, phase):
        along_y = (q < 2) == (phase == 1)
        return dev(x, ry(y + sg[d]), z, c) if along_y else dev(rx(x + sg[d]), y, z, c)

    def i_place(q, d, s):
        return rx(x - sg[d] * (s + 1)) if q < 2 else ry(y - sg[d] * (s + 1))

    def i_step(j):
        for n in both:
            for q in range(4):
                d = q % 2
                mine = ee.at[q, sub(n), :, pl.ds(j * Q, Q)]
                if j == 0:
                    send(mine, recv1.at[q, 0, sub(n)], ("i", q, 0, n), i_dev(q, d, 1))
                    continue
                here = recv1.at[q, j - 1, sub(n)]
                got(here, ("i", q, j - 1, n))
                here[...] += mine[...]
                if j < 3:
                    send(here, recv1.at[q, j, sub(n)], ("i", q, j, n), i_dev(q, d, 1))

    def i_last(s):
        for q in range(4):
            d = q % 2
            mine = recv1.at[q, 2, i_place(q, d, s)]
            if s == 0:
                send(mine, recv2.at[q, 0], ("j", q, 0), i_dev(q, d, 2))
                continue
            here = recv2.at[q, s - 1]
            got(here, ("j", q, s - 1))
            if s < 3:
                here[...] += mine[...]
                send(here, recv2.at[q, s], ("j", q, s), i_dev(q, d, 2))
            else:
                dimg_ref[:, q * Q:(q + 1) * Q] = ((here[...] + mine[...]) * scale).astype(BF16)

    def t_mine(d, s):
        return ee.at[d * 2 + c, :, :, pl.ds(1024 + s * W, W)]

    def t_swap(s):
        for d in both:
            send(ee.at[d * 2 + 1 - c, :, :, pl.ds(1024 + s * W, W)], prt.at[d, s], ("w", d, s), dev(x, y, z, 1 - c))

    def t_step(s):
        for d in both:
            got(prt.at[d, s], ("w", d, s))
            mine = t_mine(d, s)
            mine[...] += prt[d, s]
        for n in both:
            for d in both:
                mine = ee.at[d * 2 + c, sub(n), :, pl.ds(1024 + s * W, W)]
                if s == 0:
                    send(mine, zrecv.at[d, 0, sub(n)], ("z", d, 0, n), dev(x, y, rz(z + sg[d]), c))
                    continue
                here = zrecv.at[d, s - 1, sub(n)]
                got(here, ("z", d, s - 1, n))
                here[...] += mine[...]
                if s < 7:
                    send(here, zrecv.at[d, s, sub(n)], ("z", d, s, n), dev(x, y, rz(z + sg[d]), c))

    def t_out(block):
        for d in both:
            for k in range(4):
                w = d * 4 + k
                dtxt_ref[:, w * W:(w + 1) * W] = (jnp.transpose(block(d, k)) * scale).astype(BF16)

    for s in range(8):
        if ZC:
            unit_t(s)
            t_swap(s)
        if XY and s % 2 == 0:
            unit_i(s // 2)
            i_step(s // 2)
        if XY and s == 6:
            i_last(0)
        if ZC:
            t_step(s)
        if s == 3:
            sc2[mzc] = shared(sc1, "m", plane, plane_slot)
            share(sc2, "n", line, mzc, to_line)
    if XY:
        for s in range(1, 4):
            i_last(s)
    else:
        for q in range(4):
            rhs = tall[:, :, :, q * Q:(q + 1) * Q].reshape(NT * W, Q)
            res = jnp.dot(gb[0, 0], rhs, preferred_element_type=F32)
            dimg_ref[:, q * Q:(q + 1) * Q] = (res * scale).astype(BF16)
    if ZC:
        t_out(lambda d, k: zrecv[d, 6, k])
    else:
        for d in both:
            res = jnp.dot(imgt[d], gb[...].reshape(NI * W, W), preferred_element_type=F32)
            for k in range(4):
                w = d * 4 + k
                dtxt_ref[:, w * W:(w + 1) * W] = (jnp.transpose(res[k * W:(k + 1) * W]) * scale).astype(BF16)
    total = shared(sc2, "n", line, line_slot)
    scal_ref[...] = jnp.broadcast_to(jnp.sum(total, axis=1, keepdims=True), (8, W))
    for copy in sends:
        copy.wait_send()


def call(NX, NY, NZ, NC, scale, img, txt):
    D = img.shape[1]
    NI, NT = NX * NY, NZ * NC
    H, Q = D // 2, D // 4
    vmem = pltpu.VMEM
    return pl.pallas_call(
        functools.partial(kernel, NX, NY, NZ, NC),
        out_shape=(jax.ShapeDtypeStruct(img.shape, BF16), jax.ShapeDtypeStruct(txt.shape, BF16),
                   jax.ShapeDtypeStruct((8, W), F32)),
        in_specs=[pl.BlockSpec(memory_space=pltpu.SMEM)] + [pl.BlockSpec(memory_space=vmem)] * 2,
        out_specs=[pl.BlockSpec(memory_space=vmem)] * 3,
        scratch_shapes=[
            vmem((NX, NY, W, D), BF16), vmem((NZ, NC, W, D), BF16), vmem((2, H, NI * W), BF16),
            vmem((4, 4, W, 2048), F32), vmem((NX, NY, W, NT * W), BF16),
            vmem((NX, NY, W, W), F32), vmem((NX, NY, W, W), F32), vmem((8, NT * W), F32), vmem((8, NT * W), F32),
            vmem((NI, NI, W), F32), vmem((NT, NT, W), F32), vmem((NI, W), F32), vmem((NT, W), F32),
            vmem((NX, NY, W, W), F32), vmem((NI, 8, W), F32), vmem((NT, 8, W), F32),
            vmem((4, 3, 4, W, Q), F32), vmem((4, 3, W, Q), F32),
            vmem((2, 8, 4, W, W), F32), vmem((2, 7, 4, W, W), F32),
            pltpu.SemaphoreType.DMA((N_SEM,)), pltpu.SemaphoreType.DMA((N_SEM,)),
        ],
        compiler_params=pltpu.CompilerParams(collective_id=0, has_side_effects=True, vmem_limit_bytes=67043328),
    )(scale, img, txt)


SHAPE = (4, 4, 8, 2)


def solution(mesh):
    batch_spec = P(("row", "col"), None)

    def local_tile(img_loc, txt_loc, log_scale):
        scale = jnp.exp(log_scale).reshape(1, 1)
        d_img, d_txt, scal = call(*SHAPE, scale, img_loc, txt_loc)
        return scal[0, 0], d_img, d_txt, scal[1, 0]

    return jax.shard_map(local_tile, mesh=mesh, in_specs=(batch_spec, batch_spec, P()),
                         out_specs=(P(), batch_spec, batch_spec, P()), check_vma=False)
```

time: 795 us -> 129 us (0.16)
  the two profiles are of different devices: /device:TPU:1 before, /device:TPU:4 now
where the time goes in v1:
time: 129 us
  Pallas kernels  123 us (95%)
  local copies, waits for them, and re-layouts  3.69 us (3%)
  between operations  1.33 us (1%)
    pallas_call x1, Pallas kernels, call(): pl.pallas_call(functools.partial(kernel, NX, NY, NZ, NC), out_shape=(jax....  123 us

profile of v1, /device:TPU:4, one launch (start us, length us, event | category | flops | bytes accessed | tf_op | source)
XLA Modules:
  0.0 128.5 jit_solution(4539019699463419673)
XLA Ops:
  1.3 123.5 %shard_map.66 = (bf16[128,1024]{1,0:T(8,128)(2,1)}, bf16[128,1024]{1,0:T(8,128)(2,1)}, f32[8,128]{1,0:T(8,128)}) custom-call(f32[1,1]{1,0:T(1,128)} %bitcast.scale_ref, bf16[128,1024]{1,0:T(8,128)(2,1)} %img_ref.1, bf16[128,1024]{1,0:T(8,128)(2,1)} %txt_ref.1), custom_call_target="tpu_custom_call" | custom-call | tf_op jit(solution)/shard_map/pallas_call | solution.py:444
  124.8 1.3 fusion
  126.1 0.0 copy-start
  126.1 1.7 %copy.10 = bf16[128,1024]{1,0:T(8,128)(2,1)} copy(bf16[128,1024]{1,0:T(8,128)(2,1)} %get-tuple-element.17) | data formatting | bytes 524288
  127.8 0.0 copy-done
  127.8 0.7 copy.11
Async XLA Ops:
  126.1 1.7 %copy-start = (bf16[128,1024]{1,0:T(8,128)(2,1)S(1)}, bf16[128,1024]{1,0:T(8,128)(2,1)}, u32[]{:S(2)}) copy-start(bf16[128,1024]{1,0:T(8,128)(2,1)} %get-tuple-element.18) | copy-start | bytes 786436

commit v2 on v0

v2 whole, which is shorter than its diff:
```python
import functools

import jax
import jax.numpy as jnp
from jax import lax
from jax.experimental import pallas as pl
from jax.experimental.pallas import tpu as pltpu
from jax.sharding import PartitionSpec as P

MESH = pl.DeviceIdType.MESH
F32 = jnp.float32
LOG2E = 1.4426950408889634
BF16 = jnp.bfloat16
W = 128


N_SEND, N_RECV = 14, 198


class Names:
    def __init__(self):
        self.ids = {}

    def __call__(self, *key):
        return self.ids.setdefault(key, len(self.ids))


def block_of(tiles):
    for a in range(1, 5):
        for b in range(1, 5):
            for r in range(1, 17):
                if tiles % (a * b * r) == 0 and tiles // (a * b * r) <= 16:
                    return a, b, r * 8, tiles // (a * b * r) * 128
    raise ValueError(tiles)


def kernel(NX, NY, NZ, NC, scale_ref, img_ref, txt_ref, dimg_ref, dtxt_ref, scal_ref,
           iall, tall, imgt, ee, gb, rsum, rel, csum, cel, rall, call_, uref, vref, ub, sc1, sc2,
           recv1, recv2, prt, zrecv, lead, ssem, rsem):
    D = img_ref.shape[1]
    NI, NT = NX * NY, NZ * NC
    XY, ZC = NI > 1, NT > 1
    H, Q = D // 2, D // 4
    inv = 1.0 / (2.0 * W * NI * NT)
    row, col = lax.axis_index("row"), lax.axis_index("col")
    x, c = lax.div(row, NC), lax.rem(row, NC)
    z, y = lax.div(col, NY), lax.rem(col, NY)
    mxy, mzc = x * NY + y, z * NC + c
    scale = scale_ref[0, 0]
    scale2 = scale * LOG2E
    rx = lambda v: lax.rem(v + 2 * NX, NX)
    ry = lambda v: lax.rem(v + 2 * NY, NY)
    rz = lambda v: lax.rem(v + 2 * NZ, NZ)

    def dev(px, py, pz, pc):
        return (pz * NY + py, px * NC + pc)

    plane = [(p, rx(x + p // NY), ry(y + p % NY)) for p in range(1, NI)]
    line = [(p, rz(z + p // NC), lax.rem(c + p % NC, NC)) for p in range(1, NT)]
    barrier = pltpu.get_barrier_semaphore()
    greet = []
    if XY:
        greet += [dev(rx(x + k), y, z, c) for k in (1, -1)] + [dev(x, ry(y + k), z, c) for k in (1, -1)]
    if ZC:
        greet += [dev(x, y, rz(z + k), c) for k in (1, -1)] + [dev(x, y, z, 1 - c)]
    for device in greet:
        pl.semaphore_signal(barrier, inc=1, device_id=device, device_id_type=MESH)
    iall[x, y] = img_ref[...]
    tall[z, c] = txt_ref[...]
    for ref in (csum, cel, rsum, rel):
        ref[...] = jnp.zeros_like(ref)
    with jax.named_scope("barrier"):
        pl.semaphore_wait(barrier, len(greet))

    rid, sid = Names(), Names()
    sent = {}
    times = [1]

    def send(src, dst, key, device, group, offset=0):
        pltpu.make_async_remote_copy(
            src_ref=src, dst_ref=dst, send_sem=ssem.at[sid(group)], recv_sem=rsem.at[rid(*key) + offset],
            device_id=device, device_id_type=MESH).start()
        size = jnp.dtype(src.dtype).itemsize
        for n in src.shape:
            size *= n
        sent[group] = sent.get(group, 0) + size * times[0]

    def got(dst, key):
        pltpu.make_async_remote_copy(
            src_ref=dst, dst_ref=dst, send_sem=ssem.at[0], recv_sem=rsem.at[rid(*key)],
            device_id=dev(x, y, z, c), device_id_type=MESH).wait_recv()

    sg = (1, -1)
    lo, full = W // 4, W // 2

    def rows(half, part=None):
        start, size = half * full, full
        if part is not None:
            start, size = start + part * lo, lo
        return pl.ds(start, size)

    def first_dev(half, d):
        return dev(rx(x + sg[d]), y, z, c) if half == 0 else dev(x, ry(y + sg[d]), z, c)

    def second_dev(half, d):
        return dev(x, ry(y + sg[d]), z, c) if half == 0 else dev(rx(x + sg[d]), y, z, c)

    def first_piece(half, off):
        return (rx(x + off), y) if half == 0 else (x, ry(y + off))

    def second_piece(half, off1, off2):
        return (rx(x + off1), ry(y + off2)) if half == 0 else (rx(x + off2), ry(y + off1))

    def ipc(pc, sl):
        return iall.at[pc[0], pc[1], sl]

    def first_send(half, d, t):
        if t == 1:
            ref = img_ref.at[rows(half)]
            send(ref, ipc((x, y), rows(half)), ("f", half, d, 1), first_dev(half, d), "f1")
        else:
            ref = ipc(first_piece(half, -sg[d]), rows(half, d))
            send(ref, ref, ("f", half, d, 2), first_dev(half, d), "f2")

    def first_got(half, d, t):
        got(ipc(first_piece(half, -sg[d] * t), rows(half) if t == 1 else rows(half, d)), ("f", half, d, t))

    def second_send(half, off, d, t):
        if t == 1:
            ref = ipc(second_piece(half, off, 0), rows(half))
            src = img_ref.at[rows(half)] if off == 0 else ref
            send(src, ref, ("s", half, off, d, 1), second_dev(half, d), "s1")
        else:
            ref = ipc(second_piece(half, off, -sg[d]), rows(half, d))
            send(ref, ref, ("s", half, off, d, 2), second_dev(half, d), "s2")

    def second_got(half, off, d, t):
        got(ipc(second_piece(half, off, -sg[d] * t), rows(half) if t == 1 else rows(half, d)), ("s", half, off, d, t))

    def t_send(d, t, h):
        ref = tall.at[rz(z - sg[d] * (t - 1)), c, rows(h)]
        src = txt_ref.at[rows(h)] if t == 1 else ref
        send(src, ref, ("t", d, t, h), dev(x, y, rz(z + sg[d]), c), "t")

    def t_got(d, t, h):
        got(tall.at[rz(z - sg[d] * t), c, rows(h)], ("t", d, t, h))

    def t_pass(off):
        if ZC:
            ref = tall.at[rz(z + off), c]
            send(txt_ref if off == 0 else ref, ref, ("p", off), dev(x, y, z, 1 - c), "p")

    def t_passed(*offs):
        if ZC:
            for off in offs:
                got(tall.at[rz(z + off), 1 - c], ("p", off))

    both = (0, 1)

    def t_round(t):
        if ZC:
            for h in both:
                for d in both:
                    t_got(d, t, h)
                    if t < 3 or h == d:
                        t_send(d, t + 1, h)
            t_pass(-t)
            t_pass(t)

    def s_round(offs, t, halves=both):
        if XY:
            for off in offs:
                for d in both:
                    for half in halves:
                        second_got(half, off, d, t)
                        if t == 1:
                            second_send(half, off, d, 2)

    CW = NC * W

    def logits(shards, zs):
        lhs = jnp.concatenate([iall[i, j] for i, j in shards], axis=0)
        for zz in zs:
            cols = pl.ds(pl.multiple_of(zz * CW, W), CW)
            rhs = tall[zz].reshape(CW, D)
            dots = lax.dot_general(lhs, rhs, (((1,), (1,)), ((), ())), preferred_element_type=F32)
            lg = dots * scale2
            e = jnp.exp2(lg)
            el = e * lg
            for n, (i, j) in enumerate(shards):
                ee[i, j, :, cols] = e[n * W:(n + 1) * W]
            for ref, val in ((rsum, e), (rel, el)):
                part = val[:, :W]
                for k in range(1, NC):
                    part = part + val[:, k * W:(k + 1) * W]
                for n, (i, j) in enumerate(shards):
                    ref[i, j] += part[n * W:(n + 1) * W]
            for ref, val in ((csum, e), (cel, el)):
                ref[:, cols] += jnp.sum(val.reshape(len(shards) * W // 8, 8, CW), axis=0)

    def near(name, *offs):
        with jax.named_scope(name):
            zs = [rz(z + off) for off in offs] if ZC else [z] if 0 in offs else []
            if not zs:
                return
            if not XY:
                logits([(x, y)], zs)
                return

            def body(g, carry):
                i = rx(x + g - 1)
                logits([(i, ry(y - 1)), (i, y), (i, ry(y + 1))], zs)
                return carry

            lax.fori_loop(0, 3, body, 0)

    def across(name, *offs):
        with jax.named_scope(name):
            zs = [rz(z + off) for off in offs] if ZC else [z] if 0 in offs else []
            if XY and zs:
                logits([(x, ry(y + 2)), (rx(x + 2), y)], zs)

    def far(name):
        with jax.named_scope(name):
            if not XY:
                return
            shards = [(rx(x - 1), ry(y + 2)), (rx(x + 1), ry(y + 2))] + [(rx(x + 2), ry(y + k)) for k in (-1, 1, 2)]
            if not ZC:
                logits(shards, [z])
                return

            def body(p, carry):
                logits(shards, [rz(z - p), rz(z + jnp.where(p == 0, 4, p))])
                return carry

            lax.fori_loop(0, 4, body, 0)

    if XY:
        for half in both:
            for d in both:
                first_send(half, d, 1)
    if ZC:
        for h in both:
            for d in both:
                t_send(d, 1, h)
        t_pass(0)
    if XY:
        for half in both:
            for d in both:
                second_send(half, 0, d, 1)
        with jax.named_scope("f1"):
            for d in both:
                for half in both:
                    first_got(half, d, 1)
                    first_send(half, d, 2)
        for d in both:
            for half in both:
                for e in both:
                    second_send(half, -sg[d], e, 1)
    with jax.named_scope("T1"):
        t_round(1)
    with jax.named_scope("s0"):
        s_round((0,), 1)
    if XY:
        with jax.named_scope("f2"):
            for d in both:
                for half in both:
                    first_got(half, d, 2)
        for half in both:
            for d in both:
                second_send(half, 2, d, 1)
    with jax.named_scope("s1"):
        s_round((-1, 1), 1)
    with jax.named_scope("T2"):
        t_round(2)
    with jax.named_scope("p1"):
        t_passed(0, -1, 1)
    near("C1", -1, 0, 1)
    with jax.named_scope("p2"):
        t_passed(-2, 2)
    near("C2", -2, 2)
    with jax.named_scope("s2"):
        s_round((2,), 1)
    with jax.named_scope("s0t2"):
        s_round((0,), 2)
    across("C3", -2, -1, 0, 1, 2)
    with jax.named_scope("T3"):
        t_round(3)
    with jax.named_scope("p3"):
        t_passed(-3, 3)
    near("C4", -3, 3)
    with jax.named_scope("T4"):
        if ZC:
            for d in both:
                t_got(d, 4, d)
            t_pass(4)
    across("C4b", -3, 3)
    with jax.named_scope("p4"):
        t_passed(4)
    near("C5", 4)
    across("C5b", 4)
    with jax.named_scope("end"):
        s_round((-1, 1), 2)
        s_round((2,), 2)
    far("C6")

    for k in range(NI):
        rall[mxy, k:k + 1, :] = jnp.sum(jnp.transpose(rsum[k // NY, k % NY]), axis=0, keepdims=True)
    for k in range(NT):
        call_[mzc, k:k + 1, :] = jnp.sum(csum[:, k * W:(k + 1) * W], axis=0, keepdims=True)

    def share(buf, key, peers, me, to):
        for p in peers:
            send(buf.at[me], buf.at[me], (key,), to(p), key)

    def shared(buf, key, peers):
        if peers:
            got(buf.at[pl.ds(0, len(peers))], (key,))
        total = buf[0]
        for k in range(1, len(peers) + 1):
            total = total + buf[k]
        return total

    to_plane = lambda p: dev(p[1], p[2], z, c)
    to_line = lambda p: dev(x, y, p[1], p[2])
    share(rall, "r", plane, mxy, to_plane)
    share(call_, "c", line, mzc, to_line)
    with jax.named_scope("imgt"):
        for k in range(NI):
            tr = jnp.transpose(iall[k // NY, k % NY])
            for d in both:
                imgt[d, :, k * W:(k + 1) * W] = tr[d * H:(d + 1) * H]
        prod = img_ref[...].astype(F32) * txt_ref[...].astype(F32)
        pos = prod[:, :W]
        for k in range(1, D // W):
            pos = pos + prod[:, k * W:(k + 1) * W]
        pos = scale * jnp.sum(pos, axis=0, keepdims=True)
    with jax.named_scope("rwait"):
        rtot = shared(rall, "r", plane)
    u = inv / rtot
    for k in range(NI):
        ub[k // NY, k % NY] = jnp.transpose(jnp.broadcast_to(u[k:k + 1, :], (W, W)))
    with jax.named_scope("cwait"):
        ctot = shared(call_, "c", line)
    v = inv / ctot
    uref[...] = rtot
    vref[...] = v

    def build(i, j):
        uu = ub[i, j]
        for k in range(NT):
            sl = slice(k * W, (k + 1) * W)
            gb[i, j, :, sl] = (ee[i, j, :, sl] * (uu + vref[k:k + 1, :])).astype(BF16)

    def builds(n, place):
        def body(k, carry):
            build(*place(k))
            return carry

        lax.fori_loop(0, n, body, 0)

    for q in range(4):
        for k in range(4):
            rid("i", q, 0, k)
    for s in range(8):
        for d in both:
            rid("w", s, d)

    def unit_t(s):
        def body(d, carry):
            zz = rz(z - (1 - 2 * d) * (s + 1))
            rhs = gb[:, :, :, pl.ds(pl.multiple_of(zz * CW, W), CW)].reshape(NI * W, CW)
            res = jnp.dot(imgt[d], rhs, preferred_element_type=F32)
            for k in range(NC):
                ee[d * 2 + k, :, :, 1024 + s * W:1024 + (s + 1) * W] = res[:, k * W:(k + 1) * W].reshape(4, W, W)
            send(ee.at[d * 2 + 1 - c, :, :, pl.ds(1024 + s * W, W)], prt.at[d, s], ("w", s, 0), dev(x, y, z, 1 - c), "w", d)
            return carry

        with jax.named_scope(f"ut{s}"):
            times[0] = 2
            lax.fori_loop(0, 2, body, 0)
            times[0] = 1

    def unit_i1(first, d, j):
        q = first * 2 + d
        step = (1 - 2 * d) * (j + 1)
        lhs = gb[:, ry(y - step)] if first == 0 else gb[rx(x - step)]
        rhs = tall[:, :, :, pl.ds(pl.multiple_of(q * Q, W), Q)].reshape(NT * W, Q)
        res = jnp.dot(lhs.reshape(4 * W, NT * W), rhs, preferred_element_type=F32)
        if j == 0:
            lead[q] = res.reshape(4, W, Q)
        else:
            ee[q, :, :, j * Q:(j + 1) * Q] = res.reshape(4, W, Q)

    def unit_i(first, j):
        def body(d, carry):
            unit_i1(first, d, j)
            return carry

        with jax.named_scope(f"ui{first}{j}"):
            lax.fori_loop(0, 2, body, 0)

    def i_dev(q, phase):
        d = q % 2
        along_y = (q < 2) == (phase == 1)
        return dev(x, ry(y + sg[d]), z, c) if along_y else dev(rx(x + sg[d]), y, z, c)

    def i_place(q, k):
        d = q % 2
        return rx(x - sg[d] * (k + 1)) if q < 2 else ry(y - sg[d] * (k + 1))

    def i_step(q, j, k):
        at = i_place(q, k)
        mine = ee.at[q, at, :, pl.ds(j * Q, Q)]
        here = recv1.at[q, j - 1, at]
        got(here, ("i", q, j - 1, k))
        here[...] += mine[...]
        if j < 3:
            send(here, recv1.at[q, j, at], ("i", q, j, k), i_dev(q, 1), "i")
        elif k == 0:
            send(here, recv2.at[q, 0], ("j", q, 0), i_dev(q, 2), "j")

    def i_last(q, s):
        mine = recv1.at[q, 2, i_place(q, s)]
        here = recv2.at[q, s - 1]
        got(here, ("j", q, s - 1))
        if s < 3:
            here[...] += mine[...]
            send(here, recv2.at[q, s], ("j", q, s), i_dev(q, 2), "j")
        else:
            dimg_ref[:, q * Q:(q + 1) * Q] = ((here[...] + mine[...]) * scale).astype(BF16)

    def z_step(d, s, k):
        if k == 0:
            got(prt.at[d, s], ("w", s, d))
        mine = ee.at[d * 2 + c, k, :, pl.ds(1024 + s * W, W)]
        if s == 0:
            mine[...] += prt[d, s, k]
            here = mine
        else:
            here = zrecv.at[d, s - 1, k]
            got(here, ("z", d, s - 1, k))
        if s == 7:
            w = d * 4 + k
            block = here[...] + (mine[...] + prt[d, s, k])
            dtxt_ref[:, w * W:(w + 1) * W] = (jnp.transpose(block) * scale).astype(BF16)
            return
        if s > 0:
            here[...] += mine[...] + prt[d, s, k]
        send(here, zrecv.at[d, s, k], ("z", d, s, k), dev(x, y, rz(z + sg[d]), c), "z")

    def totals():
        dts = jnp.zeros((8, W), F32)
        for k in range(NT):
            dts = dts + cel[:, k * W:(k + 1) * W] * vref[k:k + 1, :]

        def body(i, acc):
            for j in range(NY):
                acc = acc + jnp.sum((ub[i, j] * rel[i, j]).reshape(W // 8, 8, W), axis=0)
            return acc

        dts = lax.fori_loop(0, NX, body, dts)
        dt_part = jnp.sum(dts, axis=0, keepdims=True) * (1.0 / LOG2E) - (2.0 * inv) * pos
        loss = jnp.log(uref[pl.ds(mxy, 1), :]) - jnp.log(vref[pl.ds(mzc, 1), :] * (1.0 / inv)) - 2.0 * pos
        line_no = lax.broadcasted_iota(jnp.int32, (8, W), 0)
        sc1[mxy] = jnp.where(line_no == 0, jnp.broadcast_to(loss * inv, (8, W)),
                             jnp.where(line_no == 1, jnp.broadcast_to(dt_part, (8, W)), 0.0))
        share(sc1, "m", plane, mxy, to_plane)

    def totals2():
        sc2[mzc] = shared(sc1, "m", plane)
        share(sc2, "n", line, mzc, to_line)

    def start(d, carry):
        sign = 1 - 2 * d
        builds(4 - d, lambda k: (rx(x + k), ry(y - sign)))
        unit_i1(0, d, 0)
        for k in range(4):
            at = rx(x - sign * (k + 1))
            send(lead.at[d, at], recv1.at[d, 0, at], ("i", 0, 0, k), dev(x, ry(y + sign), z, c), "i", 4 * d)
        builds(3 - d, lambda k: (rx(x - sign), ry(y + k * (1 + d))))
        unit_i1(1, d, 0)
        for k in range(4):
            at = ry(y - sign * (k + 1))
            send(lead.at[2 + d, at], recv1.at[2 + d, 0, at], ("i", 2, 0, k), dev(rx(x + sign), y, z, c), "i", 4 * d)
        return carry

    if XY:
        with jax.named_scope("start"):
            times[0] = 2
            lax.fori_loop(0, 2, start, 0)
            times[0] = 1
        builds(4, lambda k: (rx(x + 2 * lax.div(k, 2)), ry(y + 2 * lax.rem(k, 2))))
    else:
        build(0, 0)
    own = pl.ds(pl.multiple_of(mzc * W, W), W)
    eye = lax.broadcasted_iota(jnp.int32, (W, W), 0) == lax.broadcasted_iota(jnp.int32, (W, W), 1)
    gb[x, y, :, own] = (ee[x, y, :, own] * (ub[x, y] + vref[pl.ds(mzc, 1), :])
                        - jnp.where(eye, 2.0 * inv, 0.0)).astype(BF16)
    if ZC:
        unit_t(0)

    PERIOD, LAT = 11.3, 2.0
    base = {0: 0.0, 2: 1.2, 1: 2.4, 3: 3.5}
    zbase = 6.5
    events, work = [], []
    if ZC:
        for k in range(4):
            for d in both:
                events.append((zbase + 0.01 * k, 1, ("z", d, 0, k)))
        for s in range(1, 8):
            t0 = zbase + (s - 1) * PERIOD / 2 + LAT
            work.append((t0 + PERIOD / 8, ("ut", s)))
            for k in range(4):
                for d in both:
                    events.append((t0 + (k + 1) * PERIOD / 8, 1, ("z", d, s, k)))
    if XY:
        for q in range(4):
            for j in range(1, 4):
                t0 = base[q] + (j - 1) * PERIOD + LAT + 2.5
                if q % 2 == 0:
                    work.append((t0 + PERIOD / 4, ("ui", q // 2, j)))
                for k in range(4):
                    t = t0 + (k + 1) * PERIOD / 4
                    events.append((t, 2, ("i", q, j, k)))
                    if j == 3 and k:
                        events.append((max(t, base[q] + 32.0 + 4.8 * k), 3, ("j", q, k)))
    events.append((zbase + 3.0, 0, ("totals",)))
    events.append((zbase + 20.0, 0, ("totals2",)))
    events.sort()
    work.sort()
    needs = {}
    for t, what in work:
        if what[0] == "ut":
            needs[what] = lambda e, s=what[1]: e[0] == "z" and e[2] == s
        else:
            needs[what] = lambda e, f=what[1], j=what[2]: e[0] == "i" and e[1] // 2 == f and e[2] == j
    now = 5.5
    run = {"z": z_step, "i": i_step, "j": i_last, "totals": totals, "totals2": totals2, "ut": unit_t, "ui": unit_i}
    for t, _, event in events:
        while work and (now + 1.5 <= t + 0.3 or any(needs[w](event) for _, w in work)):
            _, w = work.pop(0)
            run[w[0]](*w[1:])
            now += 1.5
        with jax.named_scope("_".join(str(v) for v in event)):
            run[event[0]](*event[1:])
        now = max(now, t) + 0.07

    if not XY:
        for q in range(4):
            rhs = tall[:, :, :, q * Q:(q + 1) * Q].reshape(NT * W, Q)
            res = jnp.dot(gb[0, 0], rhs, preferred_element_type=F32)
            dimg_ref[:, q * Q:(q + 1) * Q] = (res * scale).astype(BF16)
    if not ZC:
        for d in both:
            res = jnp.dot(imgt[d], gb[...].reshape(NI * W, W), preferred_element_type=F32)
            for k in range(4):
                w = d * 4 + k
                dtxt_ref[:, w * W:(w + 1) * W] = (jnp.transpose(res[k * W:(k + 1) * W]) * scale).astype(BF16)
    with jax.named_scope("fin"):
        total = shared(sc2, "n", line)
        scal_ref[...] = jnp.broadcast_to(jnp.sum(total, axis=1, keepdims=True), (8, W))
    for group, size in sent.items():
        a, b, r, l = block_of(size // 4096)
        ref = ee.at[pl.ds(0, a), pl.ds(0, b), pl.ds(0, r), pl.ds(0, l)]
        pltpu.make_async_remote_copy(
            src_ref=ref, dst_ref=ref, send_sem=ssem.at[sid(group)], recv_sem=rsem.at[0],
            device_id=dev(x, y, z, c), device_id_type=MESH).wait_send()
    assert len(sid.ids) <= N_SEND and len(rid.ids) <= N_RECV, (len(sid.ids), len(rid.ids))

def call(NX, NY, NZ, NC, scale, img, txt):
    D = img.shape[1]
    NI, NT = NX * NY, NZ * NC
    H, Q = D // 2, D // 4
    vmem = pltpu.VMEM
    return pl.pallas_call(
        functools.partial(kernel, NX, NY, NZ, NC),
        out_shape=(jax.ShapeDtypeStruct(img.shape, BF16), jax.ShapeDtypeStruct(txt.shape, BF16),
                   jax.ShapeDtypeStruct((8, W), F32)),
        in_specs=[pl.BlockSpec(memory_space=pltpu.SMEM)] + [pl.BlockSpec(memory_space=vmem)] * 2,
        out_specs=[pl.BlockSpec(memory_space=vmem)] * 3,
        scratch_shapes=[
            vmem((NX, NY, W, D), BF16), vmem((NZ, NC, W, D), BF16), vmem((2, H, NI * W), BF16),
            vmem((4, 4, W, 2048), F32), vmem((NX, NY, W, NT * W), BF16),
            vmem((NX, NY, W, W), F32), vmem((NX, NY, W, W), F32), vmem((8, NT * W), F32), vmem((8, NT * W), F32),
            vmem((NI, NI, W), F32), vmem((NT, NT, W), F32), vmem((NI, W), F32), vmem((NT, W), F32),
            vmem((NX, NY, W, W), F32), vmem((NI, 8, W), F32), vmem((NT, 8, W), F32),
            vmem((4, 3, 4, W, Q), F32), vmem((4, 3, W, Q), F32),
            vmem((2, 8, 4, W, W), F32), vmem((2, 7, 4, W, W), F32), vmem((4, 4, W, Q), F32),
            pltpu.SemaphoreType.DMA((N_SEND,)), pltpu.SemaphoreType.DMA((N_RECV,)),
        ],
        compiler_params=pltpu.CompilerParams(collective_id=0, has_side_effects=True, vmem_limit_bytes=67043328),
    )(scale, img, txt)


SHAPE = (4, 4, 8, 2)


def solution(mesh):
    batch_spec = P(("row", "col"), None)

    def local_tile(img_loc, txt_loc, log_scale):
        scale = jnp.exp(log_scale).reshape(1, 1)
        d_img, d_txt, scal = call(*SHAPE, scale, img_loc, txt_loc)
        return scal[0, 0], d_img, d_txt, scal[1, 0]

    return jax.shard_map(local_tile, mesh=mesh, in_specs=(batch_spec, batch_spec, P()),
                         out_specs=(P(), batch_spec, batch_spec, P()), check_vma=False)
```

time: 795 us -> 116 us (0.15)
  blocking collectives: 377 us -> 0 us
  waiting for transfers between devices: 321 us -> 0 us
  Pallas kernels: 0 us -> 111 us
  matrix products: 43.9 us -> 0 us
  other arithmetic: 27.9 us -> 0 us
  between operations: 16.3 us -> 1.33 us
    psum x3 -> x0, blocking collectives: 251 us -> none  [the longest x1 110 us: local_tile(): row_tot = lax.psum(row_part * jnp.exp(row_max - row_top), 'col')]
    reduce_scatter x2 -> x0, waiting for transfers between devices: 188 us -> none  [the longest x1 188 us: local_tile(): img_sum = lax.psum_scatter(img_part, 'col', scatter_dimension=0, tiled=True)]
    all_gather x2 -> x0, waiting for transfers between devices: 132 us -> none  [the longest x1 99.5 us: local_tile(): img_block = lax.all_gather(img_loc, 'col', tiled=True)]
    pmax x2 -> x0, blocking collectives: 125 us -> none  [the longest x1 112 us: local_tile(): row_top = lax.pmax(row_max, 'col')]
    pallas_call x0 -> x1, Pallas kernels: none -> 111 us  [call(): pl.pallas_call(functools.partial(kernel, NX, NY, NZ, NC), out_shape=(jax....]
    dot_general x3 -> x0, matrix products: 43.9 us -> none  [the longest x1 16.7 us: local_tile(): jnp.einsum('id,jd->ij', img_block, txt_block, preferred_element_type=jnp....]
    convert_element_type x3 -> x0, other arithmetic: 18 us -> none  [the longest x1 14.4 us: local_tile(): grad_bf = grad_tile.astype(jnp.bfloat16)]
    reduce_sum x2 -> x0, other arithmetic: 9.78 us -> none  [the longest x1 9.1 us: local_tile(): row_part = jnp.sum(row_exp, axis=1)]
  transfers between devices with their start and end apart: 4 -> 0, of which waited for: 3 -> 0; matrix products, arithmetic and copies ran while one was open for 2% -> 0% of each run, Pallas kernels for 0% -> 0%
where the time goes in v2:
time: 116 us
  Pallas kernels  111 us (96%)
  local copies, waits for them, and re-layouts  3.69 us (3%)
  between operations  1.33 us (1%)
    pallas_call x1, Pallas kernels, call(): pl.pallas_call(functools.partial(kernel, NX, NY, NZ, NC), out_shape=(jax....  111 us
    unnamed x4, local copies, waits for them, and re-layouts  2.42 us

profile of v2, /device:TPU:1, one launch (start us, length us, event | category | flops | bytes accessed | tf_op | source)
XLA Modules:
  0.0 116.0 jit_solution(10568518325155200792)
XLA Ops:
  1.3 111.0 %shard_map.66 = (bf16[128,1024]{1,0:T(8,128)(2,1)}, bf16[128,1024]{1,0:T(8,128)(2,1)}, f32[8,128]{1,0:T(8,128)}) custom-call(f32[1,1]{1,0:T(1,128)} %bitcast.scale_ref, bf16[128,1024]{1,0:T(8,128)(2,1)} %img_ref.1, bf16[128,1024]{1,0:T(8,128)(2,1)} %txt_ref.1), custom_call_target="tpu_custom_call" | custom-call | tf_op jit(solution)/shard_map/pallas_call | solution.py:576
  112.3 1.3 %fusion = (f32[1,1]{1,0:T(1,128)}, f32[1,1]{1,0:T(1,128)}) fusion(f32[8,128]{1,0:T(8,128)} %get-tuple-element.7), kind=kLoop, calls=%fused_computation | loop fusion | bytes 16 | tf_op jit(solution)/shard_map/slice | solution.py:605
  113.6 0.0 copy-start
  113.6 1.7 %copy.10 = bf16[128,1024]{1,0:T(8,128)(2,1)} copy(bf16[128,1024]{1,0:T(8,128)(2,1)} %get-tuple-element.17) | data formatting | bytes 524288
  115.3 0.0 copy-done
  115.3 0.7 copy.11
Async XLA Ops:
  113.6 1.7 %copy-start = (bf16[128,1024]{1,0:T(8,128)(2,1)S(1)}, bf16[128,1024]{1,0:T(8,128)(2,1)}, u32[]{:S(2)}) copy-start(bf16[128,1024]{1,0:T(8,128)(2,1)} %get-tuple-element.18) | copy-start | bytes 786436

commit v3 on v2

v3 whole, which is shorter than its diff:
```python
import functools

import jax
import jax.numpy as jnp
from jax import lax
from jax.experimental import pallas as pl
from jax.experimental.pallas import tpu as pltpu
from jax.sharding import PartitionSpec as P

MESH = pl.DeviceIdType.MESH
F32 = jnp.float32
LOG2E = 1.4426950408889634
BF16 = jnp.bfloat16
W = 128


N_SEND, N_RECV = 14, 98


class Names:
    def __init__(self):
        self.ids = {}

    def __call__(self, *key):
        return self.ids.setdefault(key, len(self.ids))


def block_of(tiles):
    for a in range(1, 5):
        for b in range(1, 5):
            for r in range(1, 17):
                if tiles % (a * b * r) == 0 and tiles // (a * b * r) <= 16:
                    return a, b, r * 8, tiles // (a * b * r) * 128
    raise ValueError(tiles)


def kernel(NX, NY, NZ, NC, scale_ref, img_ref, txt_ref, dimg_ref, dtxt_ref, scal_ref,
           iall, tall, imgt, ee, gb, rsum, rel, csum, cel, rall, call_, uref, vref, ub, sc1, sc2,
           recv1, recv2, prt, zrecv, lead, ssem, rsem, lsem):
    D = img_ref.shape[1]
    NI, NT = NX * NY, NZ * NC
    XY, ZC = NI > 1, NT > 1
    H, Q = D // 2, D // 4
    inv = 1.0 / (2.0 * W * NI * NT)
    row, col = lax.axis_index("row"), lax.axis_index("col")
    x, c = lax.div(row, NC), lax.rem(row, NC)
    z, y = lax.div(col, NY), lax.rem(col, NY)
    mxy, mzc = x * NY + y, z * NC + c
    scale = scale_ref[0, 0]
    scale2 = scale * LOG2E
    rx = lambda v: lax.rem(v + 2 * NX, NX)
    ry = lambda v: lax.rem(v + 2 * NY, NY)
    rz = lambda v: lax.rem(v + 2 * NZ, NZ)

    def dev(px, py, pz, pc):
        return (pz * NY + py, px * NC + pc)

    plane = [(p, rx(x + p // NY), ry(y + p % NY)) for p in range(1, NI)]
    line = [(p, rz(z + p // NC), lax.rem(c + p % NC, NC)) for p in range(1, NT)]
    barrier = pltpu.get_barrier_semaphore()
    greet = []
    if XY:
        greet += [dev(rx(x + k), y, z, c) for k in (1, -1)] + [dev(x, ry(y + k), z, c) for k in (1, -1)]
    if ZC:
        greet += [dev(x, y, rz(z + k), c) for k in (1, -1)] + [dev(x, y, z, 1 - c)]
    for device in greet:
        pl.semaphore_signal(barrier, inc=1, device_id=device, device_id_type=MESH)
    loads = [pltpu.make_async_copy(img_ref, iall.at[x, y], lsem.at[0]), pltpu.make_async_copy(txt_ref, tall.at[z, c], lsem.at[1])]
    for load in loads:
        load.start()
    for ref in (csum, cel, rsum, rel, sc1, sc2):
        ref[...] = jnp.zeros_like(ref)
    with jax.named_scope("barrier"):
        for load in loads:
            load.wait()
        pl.semaphore_wait(barrier, len(greet))

    rid, sid = Names(), Names()
    sent = {}
    times = [1]

    def send(src, dst, key, device, group, offset=0):
        pltpu.make_async_remote_copy(
            src_ref=src, dst_ref=dst, send_sem=ssem.at[sid(group)], recv_sem=rsem.at[rid(*key) + offset],
            device_id=device, device_id_type=MESH).start()
        size = jnp.dtype(src.dtype).itemsize
        for n in src.shape:
            size *= n
        sent[group] = sent.get(group, 0) + size * times[0]

    def got(dst, key):
        pltpu.make_async_remote_copy(
            src_ref=dst, dst_ref=dst, send_sem=ssem.at[0], recv_sem=rsem.at[rid(*key)],
            device_id=dev(x, y, z, c), device_id_type=MESH).wait_recv()

    sg = (1, -1)
    lo, full = W // 4, W // 2

    def rows(half, part=None):
        start, size = half * full, full
        if part is not None:
            start, size = start + part * lo, lo
        return pl.ds(start, size)

    def first_dev(half, d):
        return dev(rx(x + sg[d]), y, z, c) if half == 0 else dev(x, ry(y + sg[d]), z, c)

    def second_dev(half, d):
        return dev(x, ry(y + sg[d]), z, c) if half == 0 else dev(rx(x + sg[d]), y, z, c)

    def first_piece(half, off):
        return (rx(x + off), y) if half == 0 else (x, ry(y + off))

    def second_piece(half, off1, off2):
        return (rx(x + off1), ry(y + off2)) if half == 0 else (rx(x + off2), ry(y + off1))

    def ipc(pc, sl):
        return iall.at[pc[0], pc[1], sl]

    def got_images(shards, key):
        got(iall.at[0, pl.ds(0, shards)], key)

    def got_texts(shards, key):
        got(tall.at[pl.ds(0, shards), 0], key)

    def first_send(half, d, t):
        if t == 1:
            ref = ipc((x, y), rows(half))
            send(ref, ref, ("f", d), first_dev(half, d), "f1")
        else:
            ref = ipc(first_piece(half, -sg[d]), rows(half, d))
            send(ref, ref, ("f2",), first_dev(half, d), "f2")

    def second_send(half, off, d, t):
        if t == 1:
            ref = ipc(second_piece(half, off, 0), rows(half))
            send(ref, ref, ("s", abs(off), d), second_dev(half, d), "s1")
        else:
            ref = ipc(second_piece(half, off, -sg[d]), rows(half, d))
            send(ref, ref, ("s2", off == 0), second_dev(half, d), "s2")

    def t_send(d, t, h):
        ref = tall.at[rz(z - sg[d] * (t - 1)), c, rows(h)]
        send(ref, ref, ("t", t, h if t < 4 else 0), dev(x, y, rz(z + sg[d]), c), "t")

    def t_pass(off):
        if ZC:
            ref = tall.at[rz(z + off), c]
            send(ref, ref, ("p", max(abs(off), 1)), dev(x, y, z, 1 - c), "p")

    def t_passed(off):
        if ZC:
            got_texts((3, 2, 2, 1)[off - 1], ("p", off))

    both = (0, 1)

    def t_half(t, h):
        if ZC:
            with jax.named_scope(f"T{t}{h}"):
                got_texts(1, ("t", t, h))
            for d in both:
                if t < 3 or h == d:
                    t_send(d, t + 1, h)
            if h == 1:
                t_pass(-t)
                t_pass(t)

    def s_round(off):
        if XY:
            for d in both:
                got_images(2 if off == 1 else 1, ("s", off, d))
                for half in both:
                    for o in ((-1, 1) if off == 1 else (off,)):
                        second_send(half, o, d, 2)

    CW = NC * W

    def logits(shards, zs):
        lhs = jnp.concatenate([iall[i, j] for i, j in shards], axis=0)
        parts = [None, None]
        for zz in zs:
            cols = pl.ds(pl.multiple_of(zz * CW, W), CW)
            rhs = tall[zz].reshape(CW, D)
            dots = lax.dot_general(lhs, rhs, (((1,), (1,)), ((), ())), preferred_element_type=F32)
            lg = dots * scale2
            e = jnp.exp2(lg)
            el = e * lg
            for n, (i, j) in enumerate(shards):
                ee[i, j, :, cols] = e[n * W:(n + 1) * W]
            for m, (ref, val) in enumerate(((csum, e), (cel, el))):
                for k in range(NC):
                    part = val[:, k * W:(k + 1) * W]
                    parts[m] = part if parts[m] is None else parts[m] + part
                ref[:, cols] += jnp.sum(val.reshape(len(shards) * W // 8, 8, CW), axis=0)
        for ref, part in ((rsum, parts[0]), (rel, parts[1])):
            for n, (i, j) in enumerate(shards):
                ref[i, j] += part[n * W:(n + 1) * W]

    cross = [(x, y)]
    corners, across = [], []
    if XY:
        cross += [(rx(x - 1), y), (rx(x + 1), y), (x, ry(y - 1)), (x, ry(y + 1))]
        corners = [(rx(x + i), ry(y + j)) for i in (-1, 1) for j in (-1, 1)]
        across = [(x, ry(y + 2)), (rx(x + 2), y)]

    def tiles(name, shards, *offs):
        zs = [rz(z + off) for off in offs] if ZC else [z] if 0 in offs else []
        if shards and zs:
            with jax.named_scope(name):
                logits(shards, zs)

    def near(name, *offs):
        zs = [rz(z + off) for off in offs]

        def body(g, carry):
            i = rx(x + g - 1)
            logits([(i, ry(y - 1)), (i, y), (i, ry(y + 1))], zs)
            return carry

        with jax.named_scope(name):
            if ZC and XY:
                lax.fori_loop(0, 3, body, 0)
            elif ZC:
                logits(cross, zs)

    def whole(name, off):
        def body(i, carry):
            logits([(i, j) for j in range(NY)], [rz(z + off)])
            return carry

        with jax.named_scope(name):
            if ZC:
                lax.fori_loop(0, NX, body, 0)

    def far(name, pairs):
        with jax.named_scope(name):
            if not XY:
                return
            shards = [(rx(x - 1), ry(y + 2)), (rx(x + 1), ry(y + 2))] + [(rx(x + 2), ry(y + k)) for k in (-1, 1, 2)]

            def body(p, carry):
                logits(shards, [rz(z - p), rz(z + p)])
                return carry

            if not pairs:
                logits(shards, [z])
            elif ZC:
                lax.fori_loop(1, 4, body, 0)

    if XY:
        for half in both:
            for d in both:
                first_send(half, d, 1)
    if ZC:
        for h in both:
            for d in both:
                t_send(d, 1, h)
        t_pass(0)
    if XY:
        for half in both:
            for d in both:
                second_send(half, 0, d, 1)
        with jax.named_scope("f1"):
            for d in both:
                got_images(1, ("f", d))
                for half in both:
                    first_send(half, d, 2)
        for d in both:
            for half in both:
                for e in both:
                    second_send(half, -sg[d], e, 1)
    t_half(1, 0)
    t_half(1, 1)
    with jax.named_scope("s0"):
        s_round(0)
    if XY:
        with jax.named_scope("f2"):
            got_images(1, ("f2",))
        for half in both:
            for d in both:
                second_send(half, 2, d, 1)
    with jax.named_scope("p1"):
        t_passed(1)
    t_half(2, 0)
    tiles("C0", cross, -1, 0, 1)
    t_half(2, 1)
    with jax.named_scope("s1"):
        s_round(1)
    tiles("C1", corners, -1, 0, 1)
    t_half(3, 0)
    with jax.named_scope("p2"):
        t_passed(2)
    near("C2", -2, 2)
    with jax.named_scope("s0t2"):
        if XY:
            got_images(1, ("s2", True))
    tiles("C3", across, -2, -1, 0, 1, 2)
    t_half(3, 1)
    with jax.named_scope("s2"):
        s_round(2)
    with jax.named_scope("p3"):
        t_passed(3)
    near("C4", -3, 3)
    with jax.named_scope("T4"):
        if ZC:
            got_texts(1, ("t", 4, 0))
            t_pass(4)
    tiles("C4b", across, -3, 3)
    with jax.named_scope("end"):
        if XY:
            got_images(3, ("s2", False))
    far("C6", 1)
    far("C7", 0)
    with jax.named_scope("p4"):
        t_passed(4)
    whole("C5", 4)

    for k in range(NI):
        rall[mxy, k:k + 1, :] = jnp.sum(jnp.transpose(rsum[k // NY, k % NY]), axis=0, keepdims=True)
    for k in range(NT):
        call_[mzc, k:k + 1, :] = jnp.sum(csum[:, k * W:(k + 1) * W], axis=0, keepdims=True)

    def share(buf, key, peers, me, to, rows=None):
        ref = buf.at[me] if rows is None else buf.at[me, pl.ds(0, rows)]
        for p in peers:
            send(ref, ref, (key,), to(p), key)

    def shared(buf, key, peers, rows=None):
        if peers:
            ref = buf.at[pl.ds(0, len(peers))]
            got(ref if rows is None else ref.at[:, pl.ds(0, rows)], (key,))
        total = buf[0]
        for k in range(1, len(peers) + 1):
            total = total + buf[k]
        return total

    to_plane = lambda p: dev(p[1], p[2], z, c)
    to_line = lambda p: dev(x, y, p[1], p[2])
    share(rall, "r", plane, mxy, to_plane)
    share(call_, "c", line, mzc, to_line)
    with jax.named_scope("imgt"):
        for k in range(NI):
            tr = jnp.transpose(iall[k // NY, k % NY])
            for d in both:
                imgt[d, :, k * W:(k + 1) * W] = tr[d * H:(d + 1) * H]
        prod = iall[x, y].astype(F32) * tall[z, c].astype(F32)
        pos = prod[:, :W]
        for k in range(1, D // W):
            pos = pos + prod[:, k * W:(k + 1) * W]
        pos = scale * jnp.sum(pos, axis=0, keepdims=True)
    with jax.named_scope("rwait"):
        rtot = shared(rall, "r", plane)
    u = inv / rtot
    for k in range(NI):
        ub[k // NY, k % NY] = jnp.transpose(jnp.broadcast_to(u[k:k + 1, :], (W, W)))
    with jax.named_scope("cwait"):
        ctot = shared(call_, "c", line)
    v = inv / ctot
    uref[...] = rtot
    vref[...] = v

    def build(i, j):
        uu = ub[i, j]
        for k in range(NT):
            sl = slice(k * W, (k + 1) * W)
            gb[i, j, :, sl] = (ee[i, j, :, sl] * (uu + vref[k:k + 1, :])).astype(BF16)

    def builds(n, place):
        def body(k, carry):
            build(*place(k))
            return carry

        lax.fori_loop(0, n, body, 0)

    def unit_t(s):
        def body(d, carry):
            zz = rz(z - (1 - 2 * d) * (s + 1))
            rhs = gb[:, :, :, pl.ds(pl.multiple_of(zz * CW, W), CW)].reshape(NI * W, CW)
            res = jnp.dot(imgt[d], rhs, preferred_element_type=F32)
            for k in range(NC):
                ee[d * 2 + k, :, :, 1024 + s * W:1024 + (s + 1) * W] = res[:, k * W:(k + 1) * W].reshape(4, W, W)
            send(ee.at[d * 2 + 1 - c, :, :, pl.ds(1024 + s * W, W)], prt.at[d, s], ("w", s), dev(x, y, z, 1 - c), "w")
            return carry

        with jax.named_scope(f"ut{s}"):
            times[0] = 2
            lax.fori_loop(0, 2, body, 0)
            times[0] = 1

    def unit_i1(first, d, j):
        q = first * 2 + d
        step = (1 - 2 * d) * (j + 1)
        lhs = gb[:, ry(y - step)] if first == 0 else gb[rx(x - step)]
        rhs = tall[:, :, :, pl.ds(pl.multiple_of(q * Q, W), Q)].reshape(NT * W, Q)
        res = jnp.dot(lhs.reshape(4 * W, NT * W), rhs, preferred_element_type=F32)
        if j == 0:
            lead[q] = res.reshape(4, W, Q)
        else:
            ee[q, :, :, j * Q:(j + 1) * Q] = res.reshape(4, W, Q)

    def unit_i(first, j):
        def body(d, carry):
            unit_i1(first, d, j)
            return carry

        with jax.named_scope(f"ui{first}{j}"):
            lax.fori_loop(0, 2, body, 0)

    def i_dev(q, along_y, sign):
        return dev(x, ry(y + sign), z, c) if along_y else dev(rx(x + sign), y, z, c)

    def i_place(q, k):
        off = (2, sg[q % 2], -sg[q % 2], 0)[k]
        return rx(x + off) if q < 2 else ry(y + off)

    def i_step(d, j, k):
        got(recv1.at[0, 0, pl.ds(0, 2)], ("i", d, j - 1, k))
        for q in (d, d + 2):
            at, sign = i_place(q, k), sg[d]
            here = recv1.at[q, j - 1, at]
            here[...] += ee[q, at, :, j * Q:(j + 1) * Q]
            if j < 3:
                send(here, recv1.at[q, j, at], ("i", d, j, k), i_dev(q, q < 2, sign), "i")
            elif k == 0:
                send(here, recv2.at[q, 0], ("j", q, 0), i_dev(q, q >= 2, sign), "j")
            elif k == 2:
                send(here, recv2.at[q, 2], ("j", q, 2), i_dev(q, q >= 2, -sign), "j")

    def i_pass(q):
        here = recv2.at[q, 0]
        got(here, ("j", q, 0))
        here[...] += recv1[q, 2, i_place(q, 1)]
        send(here, recv2.at[q, 1], ("j", q, 1), i_dev(q, q >= 2, sg[q % 2]), "j")

    def i_last(q):
        got(recv2.at[q, 2], ("j", q, 2))
        got(recv2.at[q, 1], ("j", q, 1))
        block = recv1[q, 2, i_place(q, 3)] + recv2[q, 2] + recv2[q, 1]
        dimg_ref[:, q * Q:(q + 1) * Q] = (block * scale).astype(BF16)

    def z_step(s, k):
        if k == 0:
            got(prt.at[:, s], ("w", s))
        if s > 0:
            got(zrecv.at[:, s - 1, k], ("z", s - 1, k))
        for d in both:
            mine = ee.at[d * 2 + c, k, :, pl.ds(1024 + s * W, W)]
            if s == 0:
                mine[...] += prt[d, s, k]
                here = mine
            else:
                here = zrecv.at[d, s - 1, k]
            if s == 7:
                w = d * 4 + k
                block = here[...] + (mine[...] + prt[d, s, k])
                dtxt_ref[:, w * W:(w + 1) * W] = (jnp.transpose(block) * scale).astype(BF16)
                continue
            if s > 0:
                here[...] += mine[...] + prt[d, s, k]
            send(here, zrecv.at[d, s, k], ("z", s, k), dev(x, y, rz(z + sg[d]), c), "z")

    def totals():
        dts = jnp.zeros((8, W), F32)
        for k in range(NT):
            dts = dts + cel[:, k * W:(k + 1) * W] * vref[k:k + 1, :]

        def body(i, acc):
            for j in range(NY):
                acc = acc + jnp.sum((ub[i, j] * rel[i, j]).reshape(W // 8, 8, W), axis=0)
            return acc

        dts = lax.fori_loop(0, NX, body, dts)
        dt_part = jnp.sum(dts, axis=0, keepdims=True) * (1.0 / LOG2E) - (2.0 * inv) * pos
        loss = jnp.log(uref[pl.ds(mxy, 1), :]) - jnp.log(vref[pl.ds(mzc, 1), :] * (1.0 / inv)) - 2.0 * pos
        line_no = lax.broadcasted_iota(jnp.int32, (8, W), 0)
        sc1[mxy] = jnp.where(line_no == 0, jnp.broadcast_to(loss * inv, (8, W)),
                             jnp.where(line_no == 1, jnp.broadcast_to(dt_part, (8, W)), 0.0))
        share(sc1, "m", plane, mxy, to_plane, 2)

    def totals2():
        sc2[mzc] = shared(sc1, "m", plane, 2)
        share(sc2, "n", line, mzc, to_line, 2)

    def start(d):
        sign = sg[d]
        builds(4 - d, lambda k: (rx(x + k), ry(y - sign)))
        builds(3 - d, lambda k: (rx(x - sign), ry(y + k * (1 + d))))

    def start_send(d):
        for first in both:
            unit_i1(first, d, 0)
        for k in range(4):
            for q in (d, d + 2):
                place = i_place(q, k)
                send(lead.at[q, place], recv1.at[q, 0, place], ("i", d, 0, k), i_dev(q, q < 2, sg[d]), "i")

    if XY:
        with jax.named_scope("start0"):
            start(0)
            start_send(0)
        with jax.named_scope("start1"):
            start(1)
            start_send(1)
            builds(4, lambda k: (rx(x + 2 * lax.div(k, 2)), ry(y + 2 * lax.rem(k, 2))))
    else:
        build(0, 0)
    own = pl.ds(pl.multiple_of(mzc * W, W), W)
    eye = lax.broadcasted_iota(jnp.int32, (W, W), 0) == lax.broadcasted_iota(jnp.int32, (W, W), 1)
    gb[x, y, :, own] = (ee[x, y, :, own] * (ub[x, y] + vref[pl.ds(mzc, 1), :])
                        - jnp.where(eye, 2.0 * inv, 0.0)).astype(BF16)
    STEP, SUB, Z0 = 5.65, 2.82, 5.6
    base = (0.0, 2.0)
    events = []

    def at(time, fn, *args):
        events.append((time, len(events), fn, args))

    def z_time(s, k):
        return Z0 + (s - 1) * STEP + 1.7 + SUB / 2 * (k + 1) if s else Z0

    if ZC:
        for s, slot in ((0, 0.0), (1, 4.5), (2, Z0 + 0.05), (3, z_time(1, 3)), (4, z_time(2, 3)), (5, z_time(4, 1)),
                        (6, z_time(4, 3)), (7, z_time(5, 1))):
            at(slot + 0.01, unit_t, s)
        for s in range(8):
            for k in range(4):
                at(z_time(s, k), z_step, s, k)
    if XY:
        for first, slots in ((0, (Z0, z_time(1, 1), z_time(3, 1))), (1, (Z0, z_time(2, 1), z_time(3, 3)))):
            for j in range(1, 4):
                at(slots[j - 1] + 0.02, unit_i, first, j)
        for d in both:
            for j in range(1, 4):
                for k in range(4):
                    wait = (base[d] + 1.7 + (j - 1) * 2 * STEP + (k + 1) * SUB + (1.8, 2.0, 0.8)[j - 1])
                    at(max(wait, Z0 + 0.03) if j == 1 else wait, i_step, d, j, k)
            for q in (d, d + 2):
                at(base[d] + 38.5, i_pass, q)
                at(base[d] + 44.0, i_last, q)
    at(z_time(1, 1) + 0.015, totals)
    at(25.0, totals2)
    order = [(fn.__name__,) + args for _, _, fn, args in sorted(events, key=lambda e: e[:2])]
    for n, e in enumerate(order):
        if e[0] == "i_step":
            assert all(("unit_i", f, e[2]) in order[:n] for f in both)
        if e[0] == "z_step":
            assert ("unit_t", e[1]) in order[:n]
    for _, _, fn, args in sorted(events, key=lambda e: e[:2]):
        with jax.named_scope("_".join([fn.__name__] + [str(v) for v in args])):
            fn(*args)

    if not XY:
        for q in range(4):
            rhs = tall[:, :, :, q * Q:(q + 1) * Q].reshape(NT * W, Q)
            res = jnp.dot(gb[0, 0], rhs, preferred_element_type=F32)
            dimg_ref[:, q * Q:(q + 1) * Q] = (res * scale).astype(BF16)
    if not ZC:
        for d in both:
            res = jnp.dot(imgt[d], gb[...].reshape(NI * W, W), preferred_element_type=F32)
            for k in range(4):
                w = d * 4 + k
                dtxt_ref[:, w * W:(w + 1) * W] = (jnp.transpose(res[k * W:(k + 1) * W]) * scale).astype(BF16)
    with jax.named_scope("fin"):
        total = shared(sc2, "n", line, 2)
        scal_ref[...] = jnp.broadcast_to(jnp.sum(total, axis=1, keepdims=True), (8, W))
    for group, size in sent.items():
        if group in ("m", "n"):
            ref = (sc1 if group == "m" else sc2).at[pl.ds(0, size // 1024), pl.ds(0, 2)]
            pltpu.make_async_remote_copy(
                src_ref=ref, dst_ref=ref, send_sem=ssem.at[sid(group)], recv_sem=rsem.at[0],
                device_id=dev(x, y, z, c), device_id_type=MESH).wait_send()
            continue
        a, b, r, l = block_of(size // 4096)
        ref = ee.at[pl.ds(0, a), pl.ds(0, b), pl.ds(0, r), pl.ds(0, l)]
        pltpu.make_async_remote_copy(
            src_ref=ref, dst_ref=ref, send_sem=ssem.at[sid(group)], recv_sem=rsem.at[0],
            device_id=dev(x, y, z, c), device_id_type=MESH).wait_send()
    assert len(sid.ids) <= N_SEND and len(rid.ids) <= N_RECV, (len(sid.ids), len(rid.ids))

def call(NX, NY, NZ, NC, scale, img, txt):
    D = img.shape[1]
    NI, NT = NX * NY, NZ * NC
    H, Q = D // 2, D // 4
    vmem = pltpu.VMEM
    return pl.pallas_call(
        functools.partial(kernel, NX, NY, NZ, NC),
        out_shape=(jax.ShapeDtypeStruct(img.shape, BF16), jax.ShapeDtypeStruct(txt.shape, BF16),
                   jax.ShapeDtypeStruct((8, W), F32)),
        in_specs=[pl.BlockSpec(memory_space=pltpu.SMEM)] + [pl.BlockSpec(memory_space=pl.ANY)] * 2,
        out_specs=[pl.BlockSpec(memory_space=vmem)] * 3,
        scratch_shapes=[
            vmem((NX, NY, W, D), BF16), vmem((NZ, NC, W, D), BF16), vmem((2, H, NI * W), BF16),
            vmem((4, 4, W, 2048), F32), vmem((NX, NY, W, NT * W), BF16),
            vmem((NX, NY, W, W), F32), vmem((NX, NY, W, W), F32), vmem((8, NT * W), F32), vmem((8, NT * W), F32),
            vmem((NI, NI, W), F32), vmem((NT, NT, W), F32), vmem((NI, W), F32), vmem((NT, W), F32),
            vmem((NX, NY, W, W), F32), vmem((NI, 8, W), F32), vmem((NT, 8, W), F32),
            vmem((4, 3, 4, W, Q), F32), vmem((4, 3, W, Q), F32),
            vmem((2, 8, 4, W, W), F32), vmem((2, 7, 4, W, W), F32), vmem((4, 4, W, Q), F32),
            pltpu.SemaphoreType.DMA((N_SEND,)), pltpu.SemaphoreType.DMA((N_RECV,)),
            pltpu.SemaphoreType.DMA((2,)),
        ],
        compiler_params=pltpu.CompilerParams(collective_id=0, has_side_effects=True, vmem_limit_bytes=67043328),
    )(scale, img, txt)


def finish(img_ref, txt_ref, scal_ref, dimg_ref, dtxt_ref, loss_ref, dt_ref):
    dimg_ref[...] = img_ref[...]
    dtxt_ref[...] = txt_ref[...]
    loss_ref[0, 0] = scal_ref[0, 0]
    dt_ref[0, 0] = scal_ref[1, 0]


SHAPE = (4, 4, 8, 2)


def solution(mesh):
    batch_spec = P(("row", "col"), None)

    def local_tile(img_loc, txt_loc, log_scale):
        scale = jnp.exp(log_scale).reshape(1, 1)
        d_img, d_txt, scal = call(*SHAPE, scale, img_loc, txt_loc)
        vmem = pl.BlockSpec(memory_space=pltpu.VMEM)
        smem = pl.BlockSpec(memory_space=pltpu.SMEM)
        one = jax.ShapeDtypeStruct((1, 1), F32)
        d_img, d_txt, loss, d_scale = pl.pallas_call(
            finish, out_shape=(jax.ShapeDtypeStruct(d_img.shape, BF16), jax.ShapeDtypeStruct(d_txt.shape, BF16), one, one),
            in_specs=[vmem, vmem, smem], out_specs=[vmem, vmem, smem, smem])(d_img, d_txt, scal)
        return loss[0, 0], d_img, d_txt, d_scale[0, 0]

    return jax.shard_map(local_tile, mesh=mesh, in_specs=(batch_spec, batch_spec, P()),
                         out_specs=(P(), batch_spec, batch_spec, P()), check_vma=False)
```

time: 116 us -> 102 us (0.88)
  Pallas kernels: 111 us -> 101 us
  local copies, waits for them, and re-layouts: 3.69 us -> 0 us
    pallas_call x1, Pallas kernels: 111 us -> 98.8 us  [call(): pl.pallas_call(functools.partial(kernel, NX, NY, NZ, NC), out_shape=(jax....]
    unnamed x4 -> x0, local copies, waits for them, and re-layouts: 2.42 us -> none
    pallas_call x0 -> x1, Pallas kernels: none -> 1.86 us  [local_tile(): pl.pallas_call(finish, out_shape=(jax.ShapeDtypeStruct(d_img.shape, BF16)...]
    slice x1 -> x0, local copies, waits for them, and re-layouts: 1.27 us -> none  [local_tile(): return (scal[0, 0], d_img, d_txt, scal[1, 0])]
where the time goes in v3:
time: 102 us
  Pallas kernels  101 us (99%)
  between operations  1.51 us (1%)
    pallas_call x1, Pallas kernels, call(): pl.pallas_call(functools.partial(kernel, NX, NY, NZ, NC), out_shape=(jax....  98.8 us

profile of v3, /device:TPU:1, one launch (start us, length us, event | category | flops | bytes accessed | tf_op | source)
XLA Modules:
  0.0 102.2 jit_solution(18432083537197968053)
XLA Ops:
  1.3 98.8 %shard_map.66 = (bf16[128,1024]{1,0:T(8,128)(2,1)}, bf16[128,1024]{1,0:T(8,128)(2,1)}, f32[8,128]{1,0:T(8,128)}) custom-call(f32[1,1]{1,0:T(1,128)} %bitcast.scale_ref, bf16[128,1024]{1,0:T(8,128)(2,1)} %img_ref.1, bf16[128,1024]{1,0:T(8,128)(2,1)} %txt_ref.1), custom_call_target="tpu_custom_call" | custom-call | tf_op jit(solution)/shard_map/pallas_call | solution.py:585
  100.2 1.9 %shard_map.67 = (bf16[128,1024]{1,0:T(8,128)(2,1)}, bf16[128,1024]{1,0:T(8,128)(2,1)}, f32[1,1]{1,0:T(1,128)}, f32[1,1]{1,0:T(1,128)}) custom-call(bf16[128,1024]{1,0:T(8,128)(2,1)} %get-tuple-element.11.img_ref, bf16[128,1024]{1,0:T(8,128)(2,1)} %get-tuple-element.12.txt_ref, f32[8,128]{1,0:T(8,128)} %get-tuple-element.13.scal_ref), custom_call_target="tpu_custom_call" | custom-call | tf_op jit(solution)/shard_map/pallas_call | solution.py:625

commit v4 on v3

--- a/solution.py
+++ b/solution.py
@@ -57,6 +57,9 @@
 
     plane = [(p, rx(x + p // NY), ry(y + p % NY)) for p in range(1, NI)]
     line = [(p, rz(z + p // NC), lax.rem(c + p % NC, NC)) for p in range(1, NT)]
+    near_x, near_z = (lambda k: min(k, NX - k)), (lambda k: min(k, NZ - k))
+    plane.sort(key=lambda p: -near_x(p[0] // NY) - near_x(p[0] % NY))
+    line.sort(key=lambda p: -near_z(p[0] // NC) * NC - p[0] % NC)
     barrier = pltpu.get_barrier_semaphore()
     greet = []
     if XY:
@@ -143,9 +146,10 @@
         ref = tall.at[rz(z - sg[d] * (t - 1)), c, rows(h)]
         send(ref, ref, ("t", t, h if t < 4 else 0), dev(x, y, rz(z + sg[d]), c), "t")
 
-    def t_pass(off):
+    def t_pass(off, *part):
         if ZC:
             ref = tall.at[rz(z + off), c]
+            ref = ref.at[rows(*part)] if part else ref
             send(ref, ref, ("p", max(abs(off), 1)), dev(x, y, z, 1 - c), "p")
 
     def t_passed(off):
@@ -161,9 +165,8 @@
             for d in both:
                 if t < 3 or h == d:
                     t_send(d, t + 1, h)
-            if h == 1:
-                t_pass(-t)
-                t_pass(t)
+            t_pass(-t, h)
+            t_pass(t, h)
 
     def s_round(off):
         if XY:
@@ -315,11 +318,6 @@
         t_passed(4)
     whole("C5", 4)
 
-    for k in range(NI):
-        rall[mxy, k:k + 1, :] = jnp.sum(jnp.transpose(rsum[k // NY, k % NY]), axis=0, keepdims=True)
-    for k in range(NT):
-        call_[mzc, k:k + 1, :] = jnp.sum(csum[:, k * W:(k + 1) * W], axis=0, keepdims=True)
-
     def share(buf, key, peers, me, to, rows=None):
         ref = buf.at[me] if rows is None else buf.at[me, pl.ds(0, rows)]
         for p in peers:
@@ -336,8 +334,12 @@
 
     to_plane = lambda p: dev(p[1], p[2], z, c)
     to_line = lambda p: dev(x, y, p[1], p[2])
+    for k in range(NT):
+        call_[mzc, k:k + 1, :] = jnp.sum(csum[:, k * W:(k + 1) * W], axis=0, keepdims=True)
+    share(call_, "c", line, mzc, to_line)
+    for k in range(NI):
+        rall[mxy, k:k + 1, :] = jnp.sum(jnp.transpose(rsum[k // NY, k % NY]), axis=0, keepdims=True)
     share(rall, "r", plane, mxy, to_plane)
-    share(call_, "c", line, mzc, to_line)
     with jax.named_scope("imgt"):
         for k in range(NI):
             tr = jnp.transpose(iall[k // NY, k % NY])
@@ -539,27 +541,10 @@
                 at(base[d] + 44.0, i_last, q)
     at(z_time(1, 1) + 0.015, totals)
     at(25.0, totals2)
-    order = [(fn.__name__,) + args for _, _, fn, args in sorted(events, key=lambda e: e[:2])]
-    for n, e in enumerate(order):
-        if e[0] == "i_step":
-            assert all(("unit_i", f, e[2]) in order[:n] for f in both)
-        if e[0] == "z_step":
-            assert ("unit_t", e[1]) in order[:n]
     for _, _, fn, args in sorted(events, key=lambda e: e[:2]):
         with jax.named_scope("_".join([fn.__name__] + [str(v) for v in args])):
             fn(*args)
 
-    if not XY:
-        for q in range(4):
-            rhs = tall[:, :, :, q * Q:(q + 1) * Q].reshape(NT * W, Q)
-            res = jnp.dot(gb[0, 0], rhs, preferred_element_type=F32)
-            dimg_ref[:, q * Q:(q + 1) * Q] = (res * scale).astype(BF16)
-    if not ZC:
-        for d in both:
-            res = jnp.dot(imgt[d], gb[...].reshape(NI * W, W), preferred_element_type=F32)
-            for k in range(4):
-                w = d * 4 + k
-                dtxt_ref[:, w * W:(w + 1) * W] = (jnp.transpose(res[k * W:(k + 1) * W]) * scale).astype(BF16)
     with jax.named_scope("fin"):
         total = shared(sc2, "n", line, 2)
         scal_ref[...] = jnp.broadcast_to(jnp.sum(total, axis=1, keepdims=True), (8, W))

time: 102 us -> 102 us (level)
  no operation moved by 1% of the time
where the time goes in v4:
time: 102 us
  Pallas kernels  100 us (98%)
  between operations  1.51 us (1%)
    pallas_call x1, Pallas kernels, call(): pl.pallas_call(functools.partial(kernel, NX, NY, NZ, NC), out_shape=(jax....  98.4 us

profile of v4, /device:TPU:1, one launch (start us, length us, event | category | flops | bytes accessed | tf_op | source)
XLA Modules:
  0.0 101.7 jit_solution(6870446005538036071)
XLA Ops:
  1.3 98.4 %shard_map.66 = (bf16[128,1024]{1,0:T(8,128)(2,1)}, bf16[128,1024]{1,0:T(8,128)(2,1)}, f32[8,128]{1,0:T(8,128)}) custom-call(f32[1,1]{1,0:T(1,128)} %bitcast.scale_ref, bf16[128,1024]{1,0:T(8,128)(2,1)} %img_ref.1, bf16[128,1024]{1,0:T(8,128)(2,1)} %txt_ref.1), custom_call_target="tpu_custom_call" | custom-call | tf_op jit(solution)/shard_map/pallas_call | solution.py:570
  99.7 1.9 %shard_map.67 = (bf16[128,1024]{1,0:T(8,128)(2,1)}, bf16[128,1024]{1,0:T(8,128)(2,1)}, f32[1,1]{1,0:T(1,128)}, f32[1,1]{1,0:T(1,128)}) custom-call(bf16[128,1024]{1,0:T(8,128)(2,1)} %get-tuple-element.11.img_ref, bf16[128,1024]{1,0:T(8,128)(2,1)} %get-tuple-element.12.txt_ref, f32[8,128]{1,0:T(8,128)} %get-tuple-element.13.scal_ref), custom_call_target="tpu_custom_call" | custom-call | tf_op jit(solution)/shard_map/pallas_call | solution.py:610

commit v5 on v4

--- a/solution.py
+++ b/solution.py
@@ -294,26 +294,26 @@
     with jax.named_scope("p2"):
         t_passed(2)
     near("C2", -2, 2)
+    t_half(3, 1)
+    with jax.named_scope("s2"):
+        s_round(2)
     with jax.named_scope("s0t2"):
         if XY:
             got_images(1, ("s2", True))
     tiles("C3", across, -2, -1, 0, 1, 2)
-    t_half(3, 1)
-    with jax.named_scope("s2"):
-        s_round(2)
     with jax.named_scope("p3"):
         t_passed(3)
     near("C4", -3, 3)
+    tiles("C4b", across, -3, 3)
+    with jax.named_scope("end"):
+        if XY:
+            got_images(3, ("s2", False))
+    far("C7", 0)
     with jax.named_scope("T4"):
         if ZC:
             got_texts(1, ("t", 4, 0))
             t_pass(4)
-    tiles("C4b", across, -3, 3)
-    with jax.named_scope("end"):
-        if XY:
-            got_images(3, ("s2", False))
     far("C6", 1)
-    far("C7", 0)
     with jax.named_scope("p4"):
         t_passed(4)
     whole("C5", 4)

time: 102 us -> 101 us (level)
  Pallas kernels: 100 us -> 98.9 us
    pallas_call x1, Pallas kernels: 98.4 us -> 97 us  [call(): pl.pallas_call(functools.partial(kernel, NX, NY, NZ, NC), out_shape=(jax....]
where the time goes in v5:
time: 101 us; the launch traced here: 100 us
  Pallas kernels  98.9 us (98%)
  between operations  1.51 us (1%)
    pallas_call x1, Pallas kernels, call(): pl.pallas_call(functools.partial(kernel, NX, NY, NZ, NC), out_shape=(jax....  97 us

profile of v5, /device:TPU:1, one launch (start us, length us, event | category | flops | bytes accessed | tf_op | source)
XLA Modules:
  0.0 100.4 jit_solution(3526448695595203443)
XLA Ops:
  1.3 97.0 %shard_map.66 = (bf16[128,1024]{1,0:T(8,128)(2,1)}, bf16[128,1024]{1,0:T(8,128)(2,1)}, f32[8,128]{1,0:T(8,128)}) custom-call(f32[1,1]{1,0:T(1,128)} %bitcast.scale_ref, bf16[128,1024]{1,0:T(8,128)(2,1)} %img_ref.1, bf16[128,1024]{1,0:T(8,128)(2,1)} %txt_ref.1), custom_call_target="tpu_custom_call" | custom-call | tf_op jit(solution)/shard_map/pallas_call | solution.py:570
  98.4 1.9 %shard_map.67 = (bf16[128,1024]{1,0:T(8,128)(2,1)}, bf16[128,1024]{1,0:T(8,128)(2,1)}, f32[1,1]{1,0:T(1,128)}, f32[1,1]{1,0:T(1,128)}) custom-call(bf16[128,1024]{1,0:T(8,128)(2,1)} %get-tuple-element.11.img_ref, bf16[128,1024]{1,0:T(8,128)(2,1)} %get-tuple-element.12.txt_ref, f32[8,128]{1,0:T(8,128)} %get-tuple-element.13.scal_ref), custom_call_target="tpu_custom_call" | custom-call | tf_op jit(solution)/shard_map/pallas_call | solution.py:610
